TPU v7x, 8 devices: a whole 2x2x1 slice. The times are simulated.
8 devices in a mesh: data: 1 (over z), ctxo: 2 (over y), ctx: 4 (over x, core).
Axes of the slice: x: 2, y: 2, z: 1, core: 2. Of those that a mesh axis runs over, the one named last changes fastest.
Arguments:
- q_seq: bfloat16 [16, 3072, 6, 128], P('data', ('ctxo', 'ctx'))
- k_seq: bfloat16 [16, 3072, 2, 128], P('data', ('ctxo', 'ctx'))
- v_seq: bfloat16 [16, 3072, 2, 128], P('data', ('ctxo', 'ctx'))
- do_seq: bfloat16 [16, 3072, 6, 128], P('data', ('ctxo', 'ctx'))
Outputs:
- output 1: bfloat16 [16, 3072, 6, 128], P('data', ('ctxo', 'ctx'))
- output 2: bfloat16 [16, 3072, 6, 128], P('data', ('ctxo', 'ctx'))
- output 3: bfloat16 [16, 3072, 2, 128], P('data', ('ctxo', 'ctx'))
- output 4: bfloat16 [16, 3072, 2, 128], P('data', ('ctxo', 'ctx'))
All inputs are finite; a program needn't handle non-finite values.
Results may differ from a plain program's by a relative error of at most 0.0125474.
Values are sent between devices in bfloat16 or wider.
A program may use at most 1 GiB of HBM per device.

v0:
```python
import math
import jax
import jax.numpy as jnp
from jax import lax
from jax.sharding import PartitionSpec as P

CTX_AXES = ('ctxo', 'ctx')


def causal_mask(n_rows):
    row_ids = lax.broadcasted_iota(jnp.int32, (n_rows, 1, n_rows), 0)
    col_ids = lax.broadcasted_iota(jnp.int32, (n_rows, 1, n_rows), 2)
    return row_ids >= col_ids


def pair_forward(q_blk, k_blk, v_blk, key_mask):
    q_scale = 1.0 / math.sqrt(q_blk.shape[-1])
    scores = jnp.einsum('bqhgd,bkhd->bhqgk', q_blk, k_blk, preferred_element_type=jnp.float32) * q_scale
    if key_mask is not None:
        scores = jnp.where(key_mask, scores, -jnp.inf)
    row_max = jnp.max(scores, axis=-1)
    prob_blk = jnp.exp(scores - row_max[..., None])
    row_sum = jnp.sum(prob_blk, axis=-1)
    out_blk = jnp.einsum('bhqgk,bkhd->bhqgd', prob_blk.astype(jnp.bfloat16), v_blk, preferred_element_type=jnp.float32)
    return out_blk / row_sum[..., None], row_max + jnp.log(row_sum)


def merge_parts(out_a, lse_a, out_b, lse_b):
    lse_new = jnp.logaddexp(lse_a, lse_b)
    out_new = out_a * jnp.exp(lse_a - lse_new)[..., None] + out_b * jnp.exp(lse_b - lse_new)[..., None]
    return out_new, lse_new


def pair_backward(q_blk, do_blk, lse_blk, drow_blk, k_blk, v_blk, key_mask):
    q_scale = 1.0 / math.sqrt(q_blk.shape[-1])
    scores = jnp.einsum('bqhgd,bkhd->bhqgk', q_blk, k_blk, preferred_element_type=jnp.float32) * q_scale
    if key_mask is not None:
        scores = jnp.where(key_mask, scores, -jnp.inf)
    prob_blk = jnp.exp(scores - lse_blk[..., None])
    dv_part = jnp.einsum('bhqgk,bqhgd->bhkd', prob_blk.astype(jnp.bfloat16), do_blk, preferred_element_type=jnp.float32)
    prob_grad = jnp.einsum('bqhgd,bkhd->bhqgk', do_blk, v_blk, preferred_element_type=jnp.float32)
    score_grad = (prob_blk * (prob_grad - drow_blk[..., None])).astype(jnp.bfloat16)
    dq_part = jnp.einsum('bhqgk,bkhd->bhqgd', score_grad, k_blk, preferred_element_type=jnp.float32) * q_scale
    dk_part = jnp.einsum('bhqgk,bqhgd->bhkd', score_grad, q_blk, preferred_element_type=jnp.float32) * q_scale
    return dq_part, dk_part, dv_part


def solution(mesh):
    n_ctx = mesh.shape['ctxo'] * mesh.shape['ctx']
    half_ctx = n_ctx // 2
    next_perm = [(src_idx, (src_idx + 1) % n_ctx) for src_idx in range(n_ctx)]
    home_kv = [(src_idx, (src_idx - half_ctx) % n_ctx) for src_idx in range(n_ctx)]
    home_q = [(src_idx, (src_idx - half_ctx + 1) % n_ctx) for src_idx in range(n_ctx)]
    blk_spec = P('data', CTX_AXES, None, None)

    def send_next(tree_in):
        return lax.ppermute(tree_in, CTX_AXES, next_perm)

    def local_attn(q_in, k_in, v_in, do_in):
        batch_rows, chunk_len, q_heads, head_dim = q_in.shape
        kv_heads = k_in.shape[2]
        row_shape = (batch_rows, chunk_len, kv_heads, q_heads // kv_heads, head_dim)
        rank_idx = lax.axis_index(CTX_AXES)
        q_own = q_in.reshape(row_shape)
        do_own = do_in.reshape(row_shape)
        diag_mask = causal_mask(chunk_len)
        last_owner = rank_idx >= half_ctx

        own_out, own_lse = pair_forward(q_own, k_in, v_in, diag_mask)

        def fwd_step(step_idx, state_in):
            own_out, own_lse, k_buf, v_buf, q_buf, hlp_out, hlp_lse = state_in
            k_buf, v_buf, q_buf, hlp_out, hlp_lse = send_next((k_buf, v_buf, q_buf, hlp_out, hlp_lse))
            is_owner = rank_idx >= step_idx
            part_out, part_lse = pair_forward(jnp.where(is_owner, q_own, q_buf), jnp.where(is_owner, k_buf, k_in), jnp.where(is_owner, v_buf, v_in), None)
            new_out, new_lse = merge_parts(jnp.where(is_owner, own_out, hlp_out), jnp.where(is_owner, own_lse, hlp_lse), part_out, part_lse)
            own_out = jnp.where(is_owner, new_out, own_out)
            own_lse = jnp.where(is_owner, new_lse, own_lse)
            hlp_out = jnp.where(is_owner, hlp_out, new_out)
            hlp_lse = jnp.where(is_owner, hlp_lse, new_lse)
            return own_out, own_lse, k_buf, v_buf, q_buf, hlp_out, hlp_lse

        fwd_state = (own_out, own_lse, k_in, v_in, q_own, jnp.zeros_like(own_out), jnp.full_like(own_lse, -jnp.inf))
        own_out, own_lse, k_buf, v_buf, q_buf, hlp_out, hlp_lse = lax.fori_loop(1, half_ctx, fwd_step, fwd_state)
        k_buf, v_buf = send_next((k_buf, v_buf))
        part_out, part_lse = pair_forward(q_own, k_buf, v_buf, None)
        new_out, new_lse = merge_parts(own_out, own_lse, part_out, part_lse)
        own_out = jnp.where(last_owner, new_out, own_out)
        own_lse = jnp.where(last_owner, new_lse, own_lse)
        hlp_out, hlp_lse = lax.ppermute((hlp_out, hlp_lse), CTX_AXES, home_q)
        own_out, own_lse = merge_parts(own_out, own_lse, hlp_out, hlp_lse)

        drow_own = jnp.sum(jnp.swapaxes(do_own, 1, 2) * own_out, axis=-1)
        dq_own, dk_own, dv_own = pair_backward(q_own, do_own, own_lse, drow_own, k_in, v_in, diag_mask)

        def bwd_step(step_idx, state_in):
            dq_own, dk_own, dv_own, kv_bundle, q_bundle = state_in
            kv_bundle, q_bundle = send_next((kv_bundle, q_bundle))
            k_buf, v_buf, dk_buf, dv_buf = kv_bundle
            q_buf, do_buf, lse_buf, drow_buf, dq_buf = q_bundle
            is_owner = rank_idx >= step_idx
            dq_part, dk_part, dv_part = pair_backward(
                jnp.where(is_owner, q_own, q_buf), jnp.where(is_owner, do_own, do_buf),
                jnp.where(is_owner, own_lse, lse_buf), jnp.where(is_owner, drow_own, drow_buf),
                jnp.where(is_owner, k_buf, k_in), jnp.where(is_owner, v_buf, v_in), None)
            dq_own = jnp.where(is_owner, dq_own + dq_part, dq_own)
            dk_own = jnp.where(is_owner, dk_own, dk_own + dk_part)
            dv_own = jnp.where(is_owner, dv_own, dv_own + dv_part)
            kv_bundle = (k_buf, v_buf, jnp.where(is_owner, dk_buf + dk_part, dk_buf), jnp.where(is_owner, dv_buf + dv_part, dv_buf))
            q_bundle = (q_buf, do_buf, lse_buf, drow_buf, jnp.where(is_owner, dq_buf, dq_buf + dq_part))
            return dq_own, dk_own, dv_own, kv_bundle, q_bundle

        kv_bundle = (k_in, v_in, jnp.zeros_like(dk_own), jnp.zeros_like(dv_own))
        q_bundle = (q_own, do_own, own_lse, drow_own, jnp.zeros_like(dq_own))
        dq_own, dk_own, dv_own, kv_bundle, q_bundle = lax.fori_loop(1, half_ctx, bwd_step, (dq_own, dk_own, dv_own, kv_bundle, q_bundle))
        k_buf, v_buf, dk_buf, dv_buf = send_next(kv_bundle)
        dq_part, dk_part, dv_part = pair_backward(q_own, do_own, own_lse, drow_own, k_buf, v_buf, None)
        dq_own = jnp.where(last_owner, dq_own + dq_part, dq_own)
        dk_buf = jnp.where(last_owner, dk_buf + dk_part, dk_buf)
        dv_buf = jnp.where(last_owner, dv_buf + dv_part, dv_buf)
        dk_buf, dv_buf = lax.ppermute((dk_buf, dv_buf), CTX_AXES, home_kv)
        dq_buf = lax.ppermute(q_bundle[4], CTX_AXES, home_q)
        out_seq = jnp.swapaxes(own_out.astype(jnp.bfloat16), 1, 2).reshape(q_in.shape)
        dq_seq = jnp.swapaxes((dq_own + dq_buf).astype(jnp.bfloat16), 1, 2).reshape(q_in.shape)
        dk_seq = jnp.swapaxes((dk_own + dk_buf).astype(jnp.bfloat16), 1, 2)
        dv_seq = jnp.swapaxes((dv_own + dv_buf).astype(jnp.bfloat16), 1, 2)
        return out_seq, dq_seq, dk_seq, dv_seq

    return jax.shard_map(local_attn, mesh=mesh, in_specs=(blk_spec, blk_spec, blk_spec, blk_spec), out_specs=(blk_spec, blk_spec, blk_spec, blk_spec), check_vma=False)
```

profile of v0, /device:TPU:5, one launch (start us, length us, event | category | flops | bytes accessed | tf_op | source)
XLA Modules:
  0.0 4940.7 jit_solution(3042838355187458885)
XLA Ops:
  12.0 24.3 fusion.39
  61.5 30.4 broadcast_divide_fusion
  97.5 1472.5 %while.62 = (s32[]{:T(128)}, f32[16,2,384,3,128]{4,2,3,1,0:T(8,128)}, f32[16,2,384,3]{2,3,1,0:T(4,128)}, bf16[16,384,2,128]{3,1,2,0:T(8,128)(2,1)}, bf16[16,384,...) while((s32[]{:T(128)}, ...), condition=%wide.region_5.6_spmd.clone, body=%wide.region_2.5_spmd.clone.sunk | while | flops 7407169536 | bytes 488423744 | solution.py:84
  109.6 334.6 %collective-permute-done.2 = bf16[16,384,2,128]{3,1,2,0:T(8,128)(2,1)} collective-permute-done((bf16[16,384,2,128]{3,1,2,0:T(8,128)(2,1)}, bf16[16,384,2,128]{3,1,2,0:T(8,128)(2,1)}, u32[]{:S(2)}, u32[]{:S(2)}) %collective-permute-start.2) | collective-permute-done | bytes 3145760 | tf_op jit(solution)/shard_map/while/body/eval_jaxpr/ppermute | solution.py:57
  448.1 29.8 collective-permute-done.4
  481.8 24.5 multiply_reduce_fusion.2
  537.2 47.2 broadcast_select_fusion.40
  603.4 333.7 %collective-permute-done.2 = bf16[16,384,2,128]{3,1,2,0:T(8,128)(2,1)} collective-permute-done((bf16[16,384,2,128]{3,1,2,0:T(8,128)(2,1)}, bf16[16,384,2,128]{3,1,2,0:T(8,128)(2,1)}, u32[]{:S(2)}, u32[]{:S(2)}) %collective-permute-start.2) | collective-permute-done | bytes 3145760 | tf_op jit(solution)/shard_map/while/body/eval_jaxpr/ppermute | solution.py:57
  941.0 29.8 collective-permute-done.4
  974.7 24.5 multiply_reduce_fusion.2
  1030.0 47.2 broadcast_select_fusion.40
  1096.2 333.7 %collective-permute-done.2 = bf16[16,384,2,128]{3,1,2,0:T(8,128)(2,1)} collective-permute-done((bf16[16,384,2,128]{3,1,2,0:T(8,128)(2,1)}, bf16[16,384,2,128]{3,1,2,0:T(8,128)(2,1)}, u32[]{:S(2)}, u32[]{:S(2)}) %collective-permute-start.2) | collective-permute-done | bytes 3145760 | tf_op jit(solution)/shard_map/while/body/eval_jaxpr/ppermute | solution.py:57
  1433.8 29.8 collective-permute-done.4
  1467.5 24.5 multiply_reduce_fusion.2
  1522.9 47.2 broadcast_select_fusion.40
  1655.7 173.1 %collective-permute-done.14 = bf16[16,384,2,128]{3,1,2,0:T(8,128)(2,1)} collective-permute-done((bf16[16,384,2,128]{3,1,2,0:T(8,128)(2,1)}, bf16[16,384,2,128]{3,1,2,0:T(8,128)(2,1)}, u32[]{:S(2)}, u32[]{:S(2)}) %collective-permute-start.14) | collective-permute-done | bytes 3145760 | tf_op jit(solution)/shard_map/ppermute | solution.py:57
  1873.3 26.0 fusion.83
  1899.3 39.2 fusion.61
  1938.5 34.9 multiply_convert_fusion.2
  2029.6 2181.7 %while.63 = (s32[]{:T(128)}, f32[16,2,384,3,128]{4,2,3,1,0:T(8,128)}, f32[16,2,384,128]{3,2,1,0:T(8,128)}, f32[16,2,384,128]{3,2,1,0:T(8,128)}, bf16[16,384,2,12...) while((s32[]{:T(128)}, ...), condition=%wide.region_10.11_spmd.clone, body=%wide.region_9.10_spmd.clone.sunk | while | flops 18301919232 | bytes 820200000 | solution.py:115
  2029.8 130.6 %collective-permute-start.6 = (bf16[16,384,2,3,128]{4,1,3,2,0:T(8,128)(2,1)}, bf16[16,384,2,3,128]{4,1,3,2,0:T(8,128)(2,1)}, u32[]{:S(2)}, u32[]{:S(2)}) collective-permute-start(bf16[16,384,2,3,128]{4,1,3,2,0:T(8,128)(2,1)} %get-tuple-element.1076), channel_id=1, source_target_pairs={{0,1},{1,2},{2,3},{3,4},{4,5},{5,6},{6,7},{7,0}} | collective-permute-start | bytes 28311560 | tf_op jit(solution)/shard_map/while/body/eval_jaxpr/ppermute | solution.py:57
  2161.7 203.5 %collective-permute-done.8 = f32[16,2,384,3]{2,3,1,0:T(4,128)S(1)} collective-permute-done((f32[16,2,384,3]{2,3,1,0:T(4,128)}, f32[16,2,384,3]{2,3,1,0:T(4,128)S(1)}, u32[]{:S(2)}, u32[]{:S(2)}) %collective-permute-start.8) | collective-permute-done | bytes 147488 | tf_op jit(solution)/shard_map/while/body/eval_jaxpr/ppermute | solution.py:57
  2374.6 26.4 collective-permute-done.9
  2482.5 32.8 multiply_convert_fusion.4
  2515.3 189.0 %collective-permute-done.12 = f32[16,2,384,128]{3,2,1,0:T(8,128)} collective-permute-done((f32[16,2,384,128]{3,2,1,0:T(8,128)}, f32[16,2,384,128]{3,2,1,0:T(8,128)}, u32[]{:S(2)}, u32[]{:S(2)}) %collective-permute-start.12) | collective-permute-done | bytes 6291488 | tf_op jit(solution)/shard_map/while/body/eval_jaxpr/ppermute | solution.py:57
  2726.4 45.4 collective-permute-done.13
  2771.8 33.9 add_select_fusion.18
  2805.6 36.6 add_select_fusion.16
  2846.1 203.5 %collective-permute-done.8 = f32[16,2,384,3]{2,3,1,0:T(4,128)S(1)} collective-permute-done((f32[16,2,384,3]{2,3,1,0:T(4,128)}, f32[16,2,384,3]{2,3,1,0:T(4,128)S(1)}, u32[]{:S(2)}, u32[]{:S(2)}) %collective-permute-start.8) | collective-permute-done | bytes 147488 | tf_op jit(solution)/shard_map/while/body/eval_jaxpr/ppermute | solution.py:57
  3166.9 32.8 multiply_convert_fusion.4
  3199.7 189.0 %collective-permute-done.12 = f32[16,2,384,128]{3,2,1,0:T(8,128)} collective-permute-done((f32[16,2,384,128]{3,2,1,0:T(8,128)}, f32[16,2,384,128]{3,2,1,0:T(8,128)}, u32[]{:S(2)}, u32[]{:S(2)}) %collective-permute-start.12) | collective-permute-done | bytes 6291488 | tf_op jit(solution)/shard_map/while/body/eval_jaxpr/ppermute | solution.py:57
  3410.8 45.4 collective-permute-done.13
  3456.2 33.8 add_select_fusion.18
  3490.0 36.6 add_select_fusion.16
  3530.5 203.5 %collective-permute-done.8 = f32[16,2,384,3]{2,3,1,0:T(4,128)S(1)} collective-permute-done((f32[16,2,384,3]{2,3,1,0:T(4,128)}, f32[16,2,384,3]{2,3,1,0:T(4,128)S(1)}, u32[]{:S(2)}, u32[]{:S(2)}) %collective-permute-start.8) | collective-permute-done | bytes 147488 | tf_op jit(solution)/shard_map/while/body/eval_jaxpr/ppermute | solution.py:57
  3851.3 32.8 multiply_convert_fusion.4
  3884.1 189.0 %collective-permute-done.12 = f32[16,2,384,128]{3,2,1,0:T(8,128)} collective-permute-done((f32[16,2,384,128]{3,2,1,0:T(8,128)}, f32[16,2,384,128]{3,2,1,0:T(8,128)}, u32[]{:S(2)}, u32[]{:S(2)}) %collective-permute-start.12) | collective-permute-done | bytes 6291488 | tf_op jit(solution)/shard_map/while/body/eval_jaxpr/ppermute | solution.py:57
  4095.1 45.4 collective-permute-done.13
  4140.5 33.9 add_select_fusion.18
  4174.4 36.6 add_select_fusion.16
  4248.1 24.6 fusion.70
  4281.8 32.7 fusion.47
  4314.5 237.7 %collective-permute-done.21 = f32[16,2,384,128]{3,2,1,0:T(8,128)} collective-permute-done((f32[16,2,384,128]{3,2,1,0:T(8,128)}, f32[16,2,384,128]{3,2,1,0:T(8,128)}, u32[]{:S(2)}, u32[]{:S(2)}) %collective-permute-start.21) | collective-permute-done | bytes 6291488 | tf_op jit(solution)/shard_map/ppermute | solution.py:57
  4571.3 48.3 collective-permute-done.23
  4619.6 27.4 add_select_fusion.8
  4678.6 80.2 %collective-permute-done.22 = f32[16,2,384,128]{3,2,1,0:T(8,128)} collective-permute-done((f32[16,2,384,128]{3,2,1,0:T(8,128)}, f32[16,2,384,128]{3,2,1,0:T(8,128)}, u32[]{:S(2)}, u32[]{:S(2)}) %collective-permute-start.22) | collective-permute-done | bytes 6291488 | tf_op jit(solution)/shard_map/ppermute | solution.py:121
  4769.4 124.2 %collective-permute-done.24 = f32[16,2,384,128]{3,2,1,0:T(8,128)} collective-permute-done((f32[16,2,384,128]{3,2,1,0:T(8,128)}, f32[16,2,384,128]{3,2,1,0:T(8,128)}, u32[]{:S(2)}, u32[]{:S(2)}) %collective-permute-start.24) | collective-permute-done | bytes 6291488 | tf_op jit(solution)/shard_map/ppermute | solution.py:121
  4902.2 25.7 fusion.60
  (235 shorter events, 922.7 us)
Async XLA Ops:
  104.9 432.3 %collective-permute-start = (f32[16,2,384,3,128]{4,2,3,1,0:T(8,128)}, f32[16,2,384,3,128]{4,2,3,1,0:T(8,128)}, u32[]{:S(2)}, u32[]{:S(2)}) collective-permute-start(f32[16,2,384,3,128]{4,2,3,1,0:T(8,128)} %broadcast_select_fusion.36), channel_id=1, source_target_pairs={{0,1},{1,2},{2,3},{3,4},{4,5},{5,6},{6,7},{7,0}} | collective-permute-start | bytes 56623112 | tf_op jit(solution)/shard_map/while/body/eval_jaxpr/ppermute | solution.py:57
  106.7 375.2 %collective-permute-start.3 = (bf16[16,384,2,3,128]{4,1,3,2,0:T(8,128)(2,1)}, bf16[16,384,2,3,128]{4,1,3,2,0:T(8,128)(2,1)}, u32[]{:S(2)}, u32[]{:S(2)}) collective-permute-start(bf16[16,384,2,3,128]{4,1,3,2,0:T(8,128)(2,1)} %get-tuple-element.1023), channel_id=1, source_target_pairs={{0,1},{1,2},{2,3},{3,4},{4,5},{5,6},{6,7},{7,0}} | collective-permute-start | bytes 28311560 | tf_op jit(solution)/shard_map/while/body/eval_jaxpr/ppermute | solution.py:57
  106.7 337.5 %collective-permute-start.2 = (bf16[16,384,2,128]{3,1,2,0:T(8,128)(2,1)}, bf16[16,384,2,128]{3,1,2,0:T(8,128)(2,1)}, u32[]{:S(2)}, u32[]{:S(2)}) collective-permute-start(bf16[16,384,2,128]{3,1,2,0:T(8,128)(2,1)} %get-tuple-element.1021), channel_id=1, source_target_pairs={{0,1},{1,2},{2,3},{3,4},{4,5},{5,6},{6,7},{7,0}} | collective-permute-start | bytes 9437192 | tf_op jit(solution)/shard_map/while/body/eval_jaxpr/ppermute | solution.py:57
  106.7 371.2 %collective-permute-start.4 = (bf16[16,384,2,128]{3,1,2,0:T(8,128)(2,1)}, bf16[16,384,2,128]{3,1,2,0:T(8,128)(2,1)}, u32[]{:S(2)}, u32[]{:S(2)}) collective-permute-start(bf16[16,384,2,128]{3,1,2,0:T(8,128)(2,1)} %get-tuple-element.1022), channel_id=1, source_target_pairs={{0,1},{1,2},{2,3},{3,4},{4,5},{5,6},{6,7},{7,0}} | collective-permute-start | bytes 9437192 | tf_op jit(solution)/shard_map/while/body/eval_jaxpr/ppermute | solution.py:57
  107.5 425.9 %collective-permute-start.1 = (f32[16,2,384,3]{2,3,1,0:T(4,128)}, f32[16,2,384,3]{2,3,1,0:T(4,128)}, u32[]{:S(2)}, u32[]{:S(2)}) collective-permute-start(f32[16,2,384,3]{2,3,1,0:T(4,128)} %broadcast_select_fusion.37), channel_id=1, source_target_pairs={{0,1},{1,2},{2,3},{3,4},{4,5},{5,6},{6,7},{7,0}} | collective-permute-start | bytes 442376 | tf_op jit(solution)/shard_map/while/body/eval_jaxpr/ppermute | solution.py:57
  597.0 433.0 %collective-permute-start = (f32[16,2,384,3,128]{4,2,3,1,0:T(8,128)}, f32[16,2,384,3,128]{4,2,3,1,0:T(8,128)}, u32[]{:S(2)}, u32[]{:S(2)}) collective-permute-start(f32[16,2,384,3,128]{4,2,3,1,0:T(8,128)} %broadcast_select_fusion.36), channel_id=1, source_target_pairs={{0,1},{1,2},{2,3},{3,4},{4,5},{5,6},{6,7},{7,0}} | collective-permute-start | bytes 56623112 | tf_op jit(solution)/shard_map/while/body/eval_jaxpr/ppermute | solution.py:57
  599.5 375.2 %collective-permute-start.3 = (bf16[16,384,2,3,128]{4,1,3,2,0:T(8,128)(2,1)}, bf16[16,384,2,3,128]{4,1,3,2,0:T(8,128)(2,1)}, u32[]{:S(2)}, u32[]{:S(2)}) collective-permute-start(bf16[16,384,2,3,128]{4,1,3,2,0:T(8,128)(2,1)} %get-tuple-element.1023), channel_id=1, source_target_pairs={{0,1},{1,2},{2,3},{3,4},{4,5},{5,6},{6,7},{7,0}} | collective-permute-start | bytes 28311560 | tf_op jit(solution)/shard_map/while/body/eval_jaxpr/ppermute | solution.py:57
  599.5 337.5 %collective-permute-start.2 = (bf16[16,384,2,128]{3,1,2,0:T(8,128)(2,1)}, bf16[16,384,2,128]{3,1,2,0:T(8,128)(2,1)}, u32[]{:S(2)}, u32[]{:S(2)}) collective-permute-start(bf16[16,384,2,128]{3,1,2,0:T(8,128)(2,1)} %get-tuple-element.1021), channel_id=1, source_target_pairs={{0,1},{1,2},{2,3},{3,4},{4,5},{5,6},{6,7},{7,0}} | collective-permute-start | bytes 9437192 | tf_op jit(solution)/shard_map/while/body/eval_jaxpr/ppermute | solution.py:57
  599.6 371.2 %collective-permute-start.4 = (bf16[16,384,2,128]{3,1,2,0:T(8,128)(2,1)}, bf16[16,384,2,128]{3,1,2,0:T(8,128)(2,1)}, u32[]{:S(2)}, u32[]{:S(2)}) collective-permute-start(bf16[16,384,2,128]{3,1,2,0:T(8,128)(2,1)} %get-tuple-element.1022), channel_id=1, source_target_pairs={{0,1},{1,2},{2,3},{3,4},{4,5},{5,6},{6,7},{7,0}} | collective-permute-start | bytes 9437192 | tf_op jit(solution)/shard_map/while/body/eval_jaxpr/ppermute | solution.py:57
  601.2 425.0 %collective-permute-start.1 = (f32[16,2,384,3]{2,3,1,0:T(4,128)}, f32[16,2,384,3]{2,3,1,0:T(4,128)}, u32[]{:S(2)}, u32[]{:S(2)}) collective-permute-start(f32[16,2,384,3]{2,3,1,0:T(4,128)} %broadcast_select_fusion.37), channel_id=1, source_target_pairs={{0,1},{1,2},{2,3},{3,4},{4,5},{5,6},{6,7},{7,0}} | collective-permute-start | bytes 442376 | tf_op jit(solution)/shard_map/while/body/eval_jaxpr/ppermute | solution.py:57
  1089.9 433.0 %collective-permute-start = (f32[16,2,384,3,128]{4,2,3,1,0:T(8,128)}, f32[16,2,384,3,128]{4,2,3,1,0:T(8,128)}, u32[]{:S(2)}, u32[]{:S(2)}) collective-permute-start(f32[16,2,384,3,128]{4,2,3,1,0:T(8,128)} %broadcast_select_fusion.36), channel_id=1, source_target_pairs={{0,1},{1,2},{2,3},{3,4},{4,5},{5,6},{6,7},{7,0}} | collective-permute-start | bytes 56623112 | tf_op jit(solution)/shard_map/while/body/eval_jaxpr/ppermute | solution.py:57
  1092.4 375.2 %collective-permute-start.3 = (bf16[16,384,2,3,128]{4,1,3,2,0:T(8,128)(2,1)}, bf16[16,384,2,3,128]{4,1,3,2,0:T(8,128)(2,1)}, u32[]{:S(2)}, u32[]{:S(2)}) collective-permute-start(bf16[16,384,2,3,128]{4,1,3,2,0:T(8,128)(2,1)} %get-tuple-element.1023), channel_id=1, source_target_pairs={{0,1},{1,2},{2,3},{3,4},{4,5},{5,6},{6,7},{7,0}} | collective-permute-start | bytes 28311560 | tf_op jit(solution)/shard_map/while/body/eval_jaxpr/ppermute | solution.py:57
  1092.4 337.5 %collective-permute-start.2 = (bf16[16,384,2,128]{3,1,2,0:T(8,128)(2,1)}, bf16[16,384,2,128]{3,1,2,0:T(8,128)(2,1)}, u32[]{:S(2)}, u32[]{:S(2)}) collective-permute-start(bf16[16,384,2,128]{3,1,2,0:T(8,128)(2,1)} %get-tuple-element.1021), channel_id=1, source_target_pairs={{0,1},{1,2},{2,3},{3,4},{4,5},{5,6},{6,7},{7,0}} | collective-permute-start | bytes 9437192 | tf_op jit(solution)/shard_map/while/body/eval_jaxpr/ppermute | solution.py:57
  1092.5 371.2 %collective-permute-start.4 = (bf16[16,384,2,128]{3,1,2,0:T(8,128)(2,1)}, bf16[16,384,2,128]{3,1,2,0:T(8,128)(2,1)}, u32[]{:S(2)}, u32[]{:S(2)}) collective-permute-start(bf16[16,384,2,128]{3,1,2,0:T(8,128)(2,1)} %get-tuple-element.1022), channel_id=1, source_target_pairs={{0,1},{1,2},{2,3},{3,4},{4,5},{5,6},{6,7},{7,0}} | collective-permute-start | bytes 9437192 | tf_op jit(solution)/shard_map/while/body/eval_jaxpr/ppermute | solution.py:57
  1094.1 425.0 %collective-permute-start.1 = (f32[16,2,384,3]{2,3,1,0:T(4,128)}, f32[16,2,384,3]{2,3,1,0:T(4,128)}, u32[]{:S(2)}, u32[]{:S(2)}) collective-permute-start(f32[16,2,384,3]{2,3,1,0:T(4,128)} %broadcast_select_fusion.37), channel_id=1, source_target_pairs={{0,1},{1,2},{2,3},{3,4},{4,5},{5,6},{6,7},{7,0}} | collective-permute-start | bytes 442376 | tf_op jit(solution)/shard_map/while/body/eval_jaxpr/ppermute | solution.py:57
  1589.9 309.4 %collective-permute-start.17 = (f32[16,2,384,3,128]{2,4,3,1,0:T(8,128)}, f32[16,2,384,3,128]{2,4,3,1,0:T(8,128)}, u32[]{:S(2)}, u32[]{:S(2)}) collective-permute-start(f32[16,2,384,3,128]{2,4,3,1,0:T(8,128)} %copy.22), channel_id=1, source_target_pairs={{0,5},{1,6},{2,7},{3,0},{4,1},{5,2},{6,3},{7,4}} | collective-permute-start | bytes 56623112 | tf_op jit(solution)/shard_map/ppermute | solution.py:90
  1591.5 237.2 %collective-permute-start.14 = (bf16[16,384,2,128]{3,1,2,0:T(8,128)(2,1)}, bf16[16,384,2,128]{3,1,2,0:T(8,128)(2,1)}, u32[]{:S(2)}, u32[]{:S(2)}) collective-permute-start(bf16[16,384,2,128]{3,1,2,0:T(8,128)(2,1)} %get-tuple-element.536), channel_id=1, source_target_pairs={{0,1},{1,2},{2,3},{3,4},{4,5},{5,6},{6,7},{7,0}} | collective-permute-start | bytes 9437192 | tf_op jit(solution)/shard_map/ppermute | solution.py:57
  1593.4 278.2 %collective-permute-start.16 = (f32[16,2,384,3]{2,3,1,0:T(4,128)}, f32[16,2,384,3]{2,3,1,0:T(4,128)S(1)}, u32[]{:S(2)}, u32[]{:S(2)}) collective-permute-start(f32[16,2,384,3]{2,3,1,0:T(4,128)} %get-tuple-element.538), channel_id=1, source_target_pairs={{0,5},{1,6},{2,7},{3,0},{4,1},{5,2},{6,3},{7,4}} | collective-permute-start | bytes 442376 | tf_op jit(solution)/shard_map/ppermute | solution.py:90
  1598.1 301.3 %collective-permute-start.15 = (bf16[16,384,2,128]{1,3,2,0:T(8,128)(2,1)}, bf16[16,384,2,128]{1,3,2,0:T(8,128)(2,1)}, u32[]{:S(2)}, u32[]{:S(2)}) collective-permute-start(bf16[16,384,2,128]{1,3,2,0:T(8,128)(2,1)} %copy.19), channel_id=1, source_target_pairs={{0,1},{1,2},{2,3},{3,4},{4,5},{5,6},{6,7},{7,0}} | collective-permute-start | bytes 9437192 | tf_op jit(solution)/shard_map/ppermute | solution.py:57
  2029.8 411.3 %collective-permute-start.6 = (bf16[16,384,2,3,128]{4,1,3,2,0:T(8,128)(2,1)}, bf16[16,384,2,3,128]{4,1,3,2,0:T(8,128)(2,1)}, u32[]{:S(2)}, u32[]{:S(2)}) collective-permute-start(bf16[16,384,2,3,128]{4,1,3,2,0:T(8,128)(2,1)} %get-tuple-element.1076), channel_id=1, source_target_pairs={{0,1},{1,2},{2,3},{3,4},{4,5},{5,6},{6,7},{7,0}} | collective-permute-start | bytes 28311560 | tf_op jit(solution)/shard_map/while/body/eval_jaxpr/ppermute | solution.py:57
  2160.4 289.4 %collective-permute-start.10 = (bf16[16,384,2,3,128]{4,1,3,2,0:T(8,128)(2,1)}, bf16[16,384,2,3,128]{4,1,3,2,0:T(8,128)(2,1)}, u32[]{:S(2)}, u32[]{:S(2)}) collective-permute-start(bf16[16,384,2,3,128]{4,1,3,2,0:T(8,128)(2,1)} %get-tuple-element.1077), channel_id=1, source_target_pairs={{0,1},{1,2},{2,3},{3,4},{4,5},{5,6},{6,7},{7,0}} | collective-permute-start | bytes 28311560 | tf_op jit(solution)/shard_map/while/body/eval_jaxpr/ppermute | solution.py:57
  2160.4 204.8 %collective-permute-start.8 = (f32[16,2,384,3]{2,3,1,0:T(4,128)}, f32[16,2,384,3]{2,3,1,0:T(4,128)S(1)}, u32[]{:S(2)}, u32[]{:S(2)}) collective-permute-start(f32[16,2,384,3]{2,3,1,0:T(4,128)} %get-tuple-element.1079), channel_id=1, source_target_pairs={{0,1},{1,2},{2,3},{3,4},{4,5},{5,6},{6,7},{7,0}} | collective-permute-start | bytes 442376 | tf_op jit(solution)/shard_map/while/body/eval_jaxpr/ppermute | solution.py:57
  2161.0 252.1 %collective-permute-start.7 = (bf16[16,384,2,128]{3,1,2,0:T(8,128)(2,1)}, bf16[16,384,2,128]{3,1,2,0:T(8,128)(2,1)}, u32[]{:S(2)}, u32[]{:S(2)}) collective-permute-start(bf16[16,384,2,128]{3,1,2,0:T(8,128)(2,1)} %get-tuple-element.1072), channel_id=1, source_target_pairs={{0,1},{1,2},{2,3},{3,4},{4,5},{5,6},{6,7},{7,0}} | collective-permute-start | bytes 9437192 | tf_op jit(solution)/shard_map/while/body/eval_jaxpr/ppermute | solution.py:57
  2161.0 240.0 %collective-permute-start.9 = (f32[16,2,384,3]{2,3,1,0:T(4,128)}, f32[16,2,384,3]{2,3,1,0:T(4,128)S(1)}, u32[]{:S(2)}, u32[]{:S(2)}) collective-permute-start(f32[16,2,384,3]{2,3,1,0:T(4,128)} %get-tuple-element.1078), channel_id=1, source_target_pairs={{0,1},{1,2},{2,3},{3,4},{4,5},{5,6},{6,7},{7,0}} | collective-permute-start | bytes 442376 | tf_op jit(solution)/shard_map/while/body/eval_jaxpr/ppermute | solution.py:57
  2401.0 404.6 %collective-permute-start.5 = (f32[16,2,384,3,128]{4,2,3,1,0:T(8,128)}, f32[16,2,384,3,128]{4,2,3,1,0:T(8,128)}, u32[]{:S(2)}, u32[]{:S(2)}) collective-permute-start(f32[16,2,384,3,128]{4,2,3,1,0:T(8,128)} %broadcast_select_fusion.43), channel_id=1, source_target_pairs={{0,1},{1,2},{2,3},{3,4},{4,5},{5,6},{6,7},{7,0}} | collective-permute-start | bytes 56623112 | tf_op jit(solution)/shard_map/while/body/eval_jaxpr/ppermute | solution.py:57
  2413.2 291.2 %collective-permute-start.12 = (f32[16,2,384,128]{3,2,1,0:T(8,128)}, f32[16,2,384,128]{3,2,1,0:T(8,128)}, u32[]{:S(2)}, u32[]{:S(2)}) collective-permute-start(f32[16,2,384,128]{3,2,1,0:T(8,128)} %broadcast_select_fusion.46), channel_id=1, source_target_pairs={{0,1},{1,2},{2,3},{3,4},{4,5},{5,6},{6,7},{7,0}} | collective-permute-start | bytes 18874376 | tf_op jit(solution)/shard_map/while/body/eval_jaxpr/ppermute | solution.py:57
  2434.7 337.1 %collective-permute-start.13 = (f32[16,2,384,128]{3,2,1,0:T(8,128)}, f32[16,2,384,128]{3,2,1,0:T(8,128)}, u32[]{:S(2)}, u32[]{:S(2)}) collective-permute-start(f32[16,2,384,128]{3,2,1,0:T(8,128)} %broadcast_select_fusion.47), channel_id=1, source_target_pairs={{0,1},{1,2},{2,3},{3,4},{4,5},{5,6},{6,7},{7,0}} | collective-permute-start | bytes 18874376 | tf_op jit(solution)/shard_map/while/body/eval_jaxpr/ppermute | solution.py:57
  2842.2 283.3 %collective-permute-start.6 = (bf16[16,384,2,3,128]{4,1,3,2,0:T(8,128)(2,1)}, bf16[16,384,2,3,128]{4,1,3,2,0:T(8,128)(2,1)}, u32[]{:S(2)}, u32[]{:S(2)}) collective-permute-start(bf16[16,384,2,3,128]{4,1,3,2,0:T(8,128)(2,1)} %get-tuple-element.1076), channel_id=1, source_target_pairs={{0,1},{1,2},{2,3},{3,4},{4,5},{5,6},{6,7},{7,0}} | collective-permute-start | bytes 28311560 | tf_op jit(solution)/shard_map/while/body/eval_jaxpr/ppermute | solution.py:57
  2844.7 289.4 %collective-permute-start.10 = (bf16[16,384,2,3,128]{4,1,3,2,0:T(8,128)(2,1)}, bf16[16,384,2,3,128]{4,1,3,2,0:T(8,128)(2,1)}, u32[]{:S(2)}, u32[]{:S(2)}) collective-permute-start(bf16[16,384,2,3,128]{4,1,3,2,0:T(8,128)(2,1)} %get-tuple-element.1077), channel_id=1, source_target_pairs={{0,1},{1,2},{2,3},{3,4},{4,5},{5,6},{6,7},{7,0}} | collective-permute-start | bytes 28311560 | tf_op jit(solution)/shard_map/while/body/eval_jaxpr/ppermute | solution.py:57
  2844.8 204.8 %collective-permute-start.8 = (f32[16,2,384,3]{2,3,1,0:T(4,128)}, f32[16,2,384,3]{2,3,1,0:T(4,128)S(1)}, u32[]{:S(2)}, u32[]{:S(2)}) collective-permute-start(f32[16,2,384,3]{2,3,1,0:T(4,128)} %get-tuple-element.1079), channel_id=1, source_target_pairs={{0,1},{1,2},{2,3},{3,4},{4,5},{5,6},{6,7},{7,0}} | collective-permute-start | bytes 442376 | tf_op jit(solution)/shard_map/while/body/eval_jaxpr/ppermute | solution.py:57
  2845.4 257.7 %collective-permute-start.7 = (bf16[16,384,2,128]{3,1,2,0:T(8,128)(2,1)}, bf16[16,384,2,128]{3,1,2,0:T(8,128)(2,1)}, u32[]{:S(2)}, u32[]{:S(2)}) collective-permute-start(bf16[16,384,2,128]{3,1,2,0:T(8,128)(2,1)} %get-tuple-element.1072), channel_id=1, source_target_pairs={{0,1},{1,2},{2,3},{3,4},{4,5},{5,6},{6,7},{7,0}} | collective-permute-start | bytes 9437192 | tf_op jit(solution)/shard_map/while/body/eval_jaxpr/ppermute | solution.py:57
  2845.4 240.0 %collective-permute-start.9 = (f32[16,2,384,3]{2,3,1,0:T(4,128)}, f32[16,2,384,3]{2,3,1,0:T(4,128)S(1)}, u32[]{:S(2)}, u32[]{:S(2)}) collective-permute-start(f32[16,2,384,3]{2,3,1,0:T(4,128)} %get-tuple-element.1078), channel_id=1, source_target_pairs={{0,1},{1,2},{2,3},{3,4},{4,5},{5,6},{6,7},{7,0}} | collective-permute-start | bytes 442376 | tf_op jit(solution)/shard_map/while/body/eval_jaxpr/ppermute | solution.py:57
  3085.4 404.6 %collective-permute-start.5 = (f32[16,2,384,3,128]{4,2,3,1,0:T(8,128)}, f32[16,2,384,3,128]{4,2,3,1,0:T(8,128)}, u32[]{:S(2)}, u32[]{:S(2)}) collective-permute-start(f32[16,2,384,3,128]{4,2,3,1,0:T(8,128)} %broadcast_select_fusion.43), channel_id=1, source_target_pairs={{0,1},{1,2},{2,3},{3,4},{4,5},{5,6},{6,7},{7,0}} | collective-permute-start | bytes 56623112 | tf_op jit(solution)/shard_map/while/body/eval_jaxpr/ppermute | solution.py:57
  3103.1 285.6 %collective-permute-start.12 = (f32[16,2,384,128]{3,2,1,0:T(8,128)}, f32[16,2,384,128]{3,2,1,0:T(8,128)}, u32[]{:S(2)}, u32[]{:S(2)}) collective-permute-start(f32[16,2,384,128]{3,2,1,0:T(8,128)} %broadcast_select_fusion.46), channel_id=1, source_target_pairs={{0,1},{1,2},{2,3},{3,4},{4,5},{5,6},{6,7},{7,0}} | collective-permute-start | bytes 18874376 | tf_op jit(solution)/shard_map/while/body/eval_jaxpr/ppermute | solution.py:57
  3119.1 337.1 %collective-permute-start.13 = (f32[16,2,384,128]{3,2,1,0:T(8,128)}, f32[16,2,384,128]{3,2,1,0:T(8,128)}, u32[]{:S(2)}, u32[]{:S(2)}) collective-permute-start(f32[16,2,384,128]{3,2,1,0:T(8,128)} %broadcast_select_fusion.47), channel_id=1, source_target_pairs={{0,1},{1,2},{2,3},{3,4},{4,5},{5,6},{6,7},{7,0}} | collective-permute-start | bytes 18874376 | tf_op jit(solution)/shard_map/while/body/eval_jaxpr/ppermute | solution.py:57
  3526.6 283.3 %collective-permute-start.6 = (bf16[16,384,2,3,128]{4,1,3,2,0:T(8,128)(2,1)}, bf16[16,384,2,3,128]{4,1,3,2,0:T(8,128)(2,1)}, u32[]{:S(2)}, u32[]{:S(2)}) collective-permute-start(bf16[16,384,2,3,128]{4,1,3,2,0:T(8,128)(2,1)} %get-tuple-element.1076), channel_id=1, source_target_pairs={{0,1},{1,2},{2,3},{3,4},{4,5},{5,6},{6,7},{7,0}} | collective-permute-start | bytes 28311560 | tf_op jit(solution)/shard_map/while/body/eval_jaxpr/ppermute | solution.py:57
  3529.1 289.4 %collective-permute-start.10 = (bf16[16,384,2,3,128]{4,1,3,2,0:T(8,128)(2,1)}, bf16[16,384,2,3,128]{4,1,3,2,0:T(8,128)(2,1)}, u32[]{:S(2)}, u32[]{:S(2)}) collective-permute-start(bf16[16,384,2,3,128]{4,1,3,2,0:T(8,128)(2,1)} %get-tuple-element.1077), channel_id=1, source_target_pairs={{0,1},{1,2},{2,3},{3,4},{4,5},{5,6},{6,7},{7,0}} | collective-permute-start | bytes 28311560 | tf_op jit(solution)/shard_map/while/body/eval_jaxpr/ppermute | solution.py:57
  3529.2 204.8 %collective-permute-start.8 = (f32[16,2,384,3]{2,3,1,0:T(4,128)}, f32[16,2,384,3]{2,3,1,0:T(4,128)S(1)}, u32[]{:S(2)}, u32[]{:S(2)}) collective-permute-start(f32[16,2,384,3]{2,3,1,0:T(4,128)} %get-tuple-element.1079), channel_id=1, source_target_pairs={{0,1},{1,2},{2,3},{3,4},{4,5},{5,6},{6,7},{7,0}} | collective-permute-start | bytes 442376 | tf_op jit(solution)/shard_map/while/body/eval_jaxpr/ppermute | solution.py:57
  3529.8 257.7 %collective-permute-start.7 = (bf16[16,384,2,128]{3,1,2,0:T(8,128)(2,1)}, bf16[16,384,2,128]{3,1,2,0:T(8,128)(2,1)}, u32[]{:S(2)}, u32[]{:S(2)}) collective-permute-start(bf16[16,384,2,128]{3,1,2,0:T(8,128)(2,1)} %get-tuple-element.1072), channel_id=1, source_target_pairs={{0,1},{1,2},{2,3},{3,4},{4,5},{5,6},{6,7},{7,0}} | collective-permute-start | bytes 9437192 | tf_op jit(solution)/shard_map/while/body/eval_jaxpr/ppermute | solution.py:57
  3529.8 240.0 %collective-permute-start.9 = (f32[16,2,384,3]{2,3,1,0:T(4,128)}, f32[16,2,384,3]{2,3,1,0:T(4,128)S(1)}, u32[]{:S(2)}, u32[]{:S(2)}) collective-permute-start(f32[16,2,384,3]{2,3,1,0:T(4,128)} %get-tuple-element.1078), channel_id=1, source_target_pairs={{0,1},{1,2},{2,3},{3,4},{4,5},{5,6},{6,7},{7,0}} | collective-permute-start | bytes 442376 | tf_op jit(solution)/shard_map/while/body/eval_jaxpr/ppermute | solution.py:57
  3769.8 404.6 %collective-permute-start.5 = (f32[16,2,384,3,128]{4,2,3,1,0:T(8,128)}, f32[16,2,384,3,128]{4,2,3,1,0:T(8,128)}, u32[]{:S(2)}, u32[]{:S(2)}) collective-permute-start(f32[16,2,384,3,128]{4,2,3,1,0:T(8,128)} %broadcast_select_fusion.43), channel_id=1, source_target_pairs={{0,1},{1,2},{2,3},{3,4},{4,5},{5,6},{6,7},{7,0}} | collective-permute-start | bytes 56623112 | tf_op jit(solution)/shard_map/while/body/eval_jaxpr/ppermute | solution.py:57
  3787.5 285.6 %collective-permute-start.12 = (f32[16,2,384,128]{3,2,1,0:T(8,128)}, f32[16,2,384,128]{3,2,1,0:T(8,128)}, u32[]{:S(2)}, u32[]{:S(2)}) collective-permute-start(f32[16,2,384,128]{3,2,1,0:T(8,128)} %broadcast_select_fusion.46), channel_id=1, source_target_pairs={{0,1},{1,2},{2,3},{3,4},{4,5},{5,6},{6,7},{7,0}} | collective-permute-start | bytes 18874376 | tf_op jit(solution)/shard_map/while/body/eval_jaxpr/ppermute | solution.py:57
  3803.5 337.1 %collective-permute-start.13 = (f32[16,2,384,128]{3,2,1,0:T(8,128)}, f32[16,2,384,128]{3,2,1,0:T(8,128)}, u32[]{:S(2)}, u32[]{:S(2)}) collective-permute-start(f32[16,2,384,128]{3,2,1,0:T(8,128)} %broadcast_select_fusion.47), channel_id=1, source_target_pairs={{0,1},{1,2},{2,3},{3,4},{4,5},{5,6},{6,7},{7,0}} | collective-permute-start | bytes 18874376 | tf_op jit(solution)/shard_map/while/body/eval_jaxpr/ppermute | solution.py:57
  4232.6 669.5 %collective-permute-start.20 = (f32[16,2,384,3,128]{2,4,3,1,0:T(8,128)}, f32[16,2,384,3,128]{2,4,3,1,0:T(8,128)}, u32[]{:S(2)}, u32[]{:S(2)}) collective-permute-start(f32[16,2,384,3,128]{2,4,3,1,0:T(8,128)} %copy.43), channel_id=1, source_target_pairs={{0,5},{1,6},{2,7},{3,0},{4,1},{5,2},{6,3},{7,4}} | collective-permute-start | bytes 56623112 | tf_op jit(solution)/shard_map/ppermute | solution.py:122
  4237.1 315.2 %collective-permute-start.21 = (f32[16,2,384,128]{3,2,1,0:T(8,128)}, f32[16,2,384,128]{3,2,1,0:T(8,128)}, u32[]{:S(2)}, u32[]{:S(2)}) collective-permute-start(f32[16,2,384,128]{3,2,1,0:T(8,128)} %get-tuple-element.545), channel_id=1, source_target_pairs={{0,1},{1,2},{2,3},{3,4},{4,5},{5,6},{6,7},{7,0}} | collective-permute-start | bytes 18874376 | tf_op jit(solution)/shard_map/ppermute | solution.py:57
  4237.3 382.4 %collective-permute-start.23 = (f32[16,2,384,128]{3,2,1,0:T(8,128)}, f32[16,2,384,128]{3,2,1,0:T(8,128)}, u32[]{:S(2)}, u32[]{:S(2)}) collective-permute-start(f32[16,2,384,128]{3,2,1,0:T(8,128)} %get-tuple-element.547), channel_id=1, source_target_pairs={{0,1},{1,2},{2,3},{3,4},{4,5},{5,6},{6,7},{7,0}} | collective-permute-start | bytes 18874376 | tf_op jit(solution)/shard_map/ppermute | solution.py:57
  4571.3 187.4 %collective-permute-start.22 = (f32[16,2,384,128]{3,2,1,0:T(8,128)}, f32[16,2,384,128]{3,2,1,0:T(8,128)}, u32[]{:S(2)}, u32[]{:S(2)}) collective-permute-start(f32[16,2,384,128]{3,2,1,0:T(8,128)} %add_select_fusion.9), channel_id=1, source_target_pairs={{0,4},{1,5},{2,6},{3,7},{4,0},{5,1},{6,2},{7,3}} | collective-permute-start | bytes 18874376 | tf_op jit(solution)/shard_map/ppermute | solution.py:121
  4647.1 246.5 %collective-permute-start.24 = (f32[16,2,384,128]{3,2,1,0:T(8,128)}, f32[16,2,384,128]{3,2,1,0:T(8,128)}, u32[]{:S(2)}, u32[]{:S(2)}) collective-permute-start(f32[16,2,384,128]{3,2,1,0:T(8,128)} %add_select_fusion.8), channel_id=1, source_target_pairs={{0,4},{1,5},{2,6},{3,7},{4,0},{5,1},{6,2},{7,3}} | collective-permute-start | bytes 18874376 | tf_op jit(solution)/shard_map/ppermute | solution.py:121
  (29 other events, 1291.6 us)
where the time goes:
time: 4970 us; the launch traced here: 4940 us
  waiting for transfers between devices  3200 us (64%)
  matrix products  1010 us (20%)
  local copies, waits for them, and re-layouts  321 us (6%)
  other arithmetic  221 us (4%)
  starting transfers between devices  190 us (4%)
    ppermute x48, waiting for transfers between devices, send_next(): return lax.ppermute(tree_in, CTX_AXES, next_perm)  2990 us
    dot_general x5, matrix products, pair_forward(): jnp.einsum('bhqgk,bkhd->bhqgd', prob_blk.astype(jnp.bfloat16), v_blk, pre...  211 us
    ppermute x2, waiting for transfers between devices, local_attn(): dk_buf, dv_buf = lax.ppermute((dk_buf, dv_buf), CTX_AXES, home_kv)  204 us
    ppermute x48, starting transfers between devices, send_next(): return lax.ppermute(tree_in, CTX_AXES, next_perm)  184 us
    dot_general x5, matrix products, pair_backward(): jnp.einsum('bqhgd,bkhd->bhqgk', do_blk, v_blk, preferred_element_type=jnp...  166 us
    dot_general x5, matrix products, pair_backward(): jnp.einsum('bhqgk,bqhgd->bhkd', prob_blk.astype(jnp.bfloat16), do_blk, pr...  155 us
    dot_general x5, matrix products, pair_backward(): jnp.einsum('bhqgk,bkhd->bhqgd', score_grad, k_blk, preferred_element_type...  155 us
    while x51, local copies, waits for them, and re-layouts  128 us
  transfers between devices with their start and end apart: 53, of which 28 were waited for; matrix products, arithmetic and copies ran while one was open for 20% of the time, Pallas kernels for 0%

commit v1 on v0

v1 whole, which is shorter than its diff:
```python
import functools
import math
import jax
import jax.numpy as jnp
from jax import lax
from jax.experimental import pallas as pl
from jax.experimental.pallas import tpu as pltpu
from jax.sharding import PartitionSpec as P

CTX_AXES = ('ctxo', 'ctx')
MESH = pl.DeviceIdType.MESH
f32 = jnp.float32
bf16 = jnp.bfloat16
CHUNK = 768
SUB = 256


def dot(a, b):
    return jnp.dot(a, b, preferred_element_type=f32)


def fold(x, op):
    return op(x.reshape(x.shape[0] // 8, 8, x.shape[1]), axis=0)


def tile(i):
    return slice(i * SUB, (i + 1) * SUB)


def attend_chunk(c, q, do, k, v, o, dq, dk, dv, s, scale):
    kT, vT, qT, doT, sc_ref, dp_ref, oT, dqT, pb, sb = s
    score_scale = scale * math.log2(math.e)
    n_sub = CHUNK // SUB
    n_heads = q.shape[0]

    def rows(j, ki):
        return pl.ds(pl.multiple_of(j * CHUNK, CHUNK) + ki * SUB, SUB)

    def cols(ki, diag):
        return range(ki, n_sub) if diag else range(n_sub)

    lowest = tuple(jnp.full((8, SUB), -jnp.inf, f32) for _ in range(n_sub))

    def load_heads(h, b):
        for i in range(n_sub):
            qT[b, :, tile(i)] = q[h, tile(i), :].T
            doT[b, :, tile(i)] = do[h, tile(i), :].T

    def scores(j, b, m, ki, diag):
        for qi in cols(ki, diag):
            x = dot(k[rows(j, ki), :], qT[b, :, tile(qi)]) * score_scale
            if diag and ki == qi:
                key = lax.broadcasted_iota(jnp.int32, (SUB, SUB), 0)
                query = lax.broadcasted_iota(jnp.int32, (SUB, SUB), 1)
                x = jnp.where(key <= query, x, -jnp.inf)
            sc_ref[b, j, tile(ki), tile(qi)] = x
            m[qi] = jnp.maximum(m[qi], fold(x, jnp.max))

    def score_pass(b):
        def body(j, m, diag=False):
            m = list(m)
            for ki in range(n_sub):
                scores(j, b, m, ki, diag)
            return tuple(m)
        return body(c, lax.fori_loop(0, c, body, lowest), True)

    def forward_pass(b, m):
        top = [jnp.max(x, axis=0, keepdims=True) for x in m]
        oT[...] = jnp.zeros_like(oT)

        def body(j, l, diag=False):
            l, acc = list(l), [None] * n_sub

            def probs(ki):
                for qi in cols(ki, diag):
                    e = jnp.exp2(sc_ref[b, j, tile(ki), tile(qi)] - top[qi])
                    sc_ref[b, j, tile(ki), tile(qi)] = e
                    l[qi] = l[qi] + fold(e, jnp.sum)
                    pb[ki % 2, :, tile(qi)] = e.astype(bf16)

            def prob_grads(ki):
                for qi in cols(ki, diag):
                    dp_ref[j, tile(ki), tile(qi)] = dot(v[rows(j, ki), :], doT[b, :, tile(qi)])

            def outputs(ki):
                for qi in cols(ki, diag):
                    d = dot(vT[j, :, tile(ki)], pb[ki % 2, :, tile(qi)])
                    acc[qi] = d if acc[qi] is None else acc[qi] + d

            for ki in range(n_sub + 1):
                if ki < n_sub:
                    prob_grads(ki)
                    probs(ki)
                if ki:
                    outputs(ki - 1)
            for qi in range(n_sub):
                oT[:, tile(qi)] += acc[qi]
            return tuple(l)

        l = tuple(jnp.zeros((8, SUB), f32) for _ in range(n_sub))
        l = body(c, lax.fori_loop(0, c, body, l), True)
        return [1.0 / jnp.sum(x, axis=0, keepdims=True) for x in l]

    def finish_outputs(h, b, inv):
        drow = []
        for qi in range(n_sub):
            out = oT[:, tile(qi)] * inv[qi]
            drow.append(jnp.sum(out * doT[b, :, tile(qi)].astype(f32), axis=0, keepdims=True))
            o[h, tile(qi), :] = out.astype(bf16).T
        return drow

    def backward_pass(h, b, inv, drow, more):
        dqT[...] = jnp.zeros_like(dqT)

        def body(j, m, diag=False):
            m, acc = list(m), [None] * n_sub

            def score_grads(ki):
                for qi in cols(ki, diag):
                    p = sc_ref[b, j, tile(ki), tile(qi)] * inv[qi]
                    g = p * (dp_ref[j, tile(ki), tile(qi)] - drow[qi])
                    pb[ki % 2, :, tile(qi)] = p.astype(bf16)
                    sb[ki % 2, :, tile(qi)] = g.astype(bf16)

            def grads(ki):
                first = ki * SUB if diag else 0
                for qi in cols(ki, diag):
                    d = dot(kT[j, :, tile(ki)], sb[ki % 2, :, tile(qi)])
                    acc[qi] = d if acc[qi] is None else acc[qi] + d
                dv[rows(j, ki), :] += dot(pb[ki % 2, :, first:], do[h, first:, :])
                dk[rows(j, ki), :] += dot(sb[ki % 2, :, first:], q[h, first:, :])

            if more:
                scores(j, 1 - b, m, 0, diag)
            score_grads(0)
            for ki in range(1, n_sub):
                score_grads(ki)
                grads(ki - 1)
                if more:
                    scores(j, 1 - b, m, ki, diag)
            grads(n_sub - 1)
            for qi in range(n_sub):
                dqT[:, tile(qi)] += acc[qi]
            return tuple(m)

        m = body(c, lax.fori_loop(0, c, body, lowest), True)
        for qi in range(n_sub):
            dq[h, tile(qi), :] = (dqT[:, tile(qi)] * scale).astype(bf16).T
        return m

    load_heads(0, 0)
    m = score_pass(0)
    for h in range(n_heads):
        b = h % 2
        inv = forward_pass(b, m)
        drow = finish_outputs(h, b, inv)
        if h + 1 < n_heads:
            load_heads(h + 1, 1 - b)
        m = backward_pass(h, b, inv, drow, h + 1 < n_heads)


def kernel(n_dev, q, k, v, do, o, dq, dk, dv, qg, kg, vg, dog,
           q_v, do_v, k_v, v_v, o_v, dq_v, dk_v, dv_v, dka, dva,
           kT, vT, qT, doT, sc_ref, dp_ref, oT, dqT, pb, sb,
           in_send, in_recv, out_send, out_recv, load_sem, g_send):
    me = lax.axis_index('ctxo') * lax.axis_size('ctx') + lax.axis_index('ctx')
    n_in = lax.axis_size('ctx')
    n_rows, n_heads, blk, dim = q.shape
    n_kv = k.shape[1]
    grp = n_heads // n_kv
    own = n_rows // n_dev
    scale = 1.0 / math.sqrt(dim)
    n_chunks = n_dev * blk // CHUNK
    per_chunk = CHUNK // blk

    def where(dev):
        return (0, dev // n_in, dev % n_in)

    barrier = pltpu.get_barrier_semaphore()
    for d in range(1, n_dev):
        pl.semaphore_signal(barrier, inc=1, device_id=where((me + d) % n_dev), device_id_type=MESH)
    pl.semaphore_wait(barrier, n_dev - 1)

    arrays = ((q, qg, grp), (do, dog, grp), (k, kg, 1), (v, vg, 1))

    def send_unit(u, _):
        r, g = u // n_kv, u % n_kv
        for d in range(1, n_dev):
            peer = (me + d) % n_dev
            for a, (src, dst, w) in enumerate(arrays):
                pltpu.make_async_remote_copy(
                    src.at[own * peer + r, pl.ds(g * w, w)],
                    dst.at[u, :, pl.ds(pl.multiple_of(me * blk, blk), blk), :],
                    in_send.at[a], in_recv.at[u, a],
                    device_id=where(peer), device_id_type=MESH).start()
        return 0
    n_units = own * n_kv
    lax.fori_loop(0, n_units, send_unit, 0)

    vm = (q_v, do_v, k_v, v_v)

    def load_unit(u):
        r, g = u // n_kv, u % n_kv
        for a, (src, dst, w) in enumerate(arrays):
            got = dst.at[u, :, pl.ds(0, (n_dev - 1) * blk), :]
            pltpu.make_async_copy(got, got, in_recv.at[u, a]).wait()

        def one(s, start):
            for a, (src, dst, w) in enumerate(arrays):
                at = pl.ds(pl.multiple_of(s * blk, blk), blk)
                here = vm[a].at[:, at, :]

                @pl.when(s == me)
                def _():
                    cp = pltpu.make_async_copy(src.at[own * me + r, pl.ds(g * w, w)], here, load_sem.at[a, s])
                    cp.start() if start else cp.wait()

                @pl.when(s != me)
                def _():
                    cp = pltpu.make_async_copy(dst.at[u, :, at, :], here, load_sem.at[a, s])
                    cp.start() if start else cp.wait()
            return 0
        lax.fori_loop(0, n_dev, lambda s, _: one(s, True), 0)
        lax.fori_loop(0, n_dev, lambda s, _: one(s, False), 0)

    def place(src, dst_of, dev, send_sem, recv_sem):
        @pl.when(dev == me)
        def _():
            pltpu.make_async_copy(src, dst_of, send_sem).start()

        @pl.when(dev != me)
        def _():
            pltpu.make_async_remote_copy(src, dst_of, send_sem, recv_sem,
                                         device_id=where(dev), device_id_type=MESH).start()

    def unit(u, _):
        r, g = u // n_kv, u % n_kv
        row = own * me + r
        load_unit(u)
        for j in range(n_chunks):
            kT[j] = k_v[0, j * CHUNK:(j + 1) * CHUNK, :].T
            vT[j] = v_v[0, j * CHUNK:(j + 1) * CHUNK, :].T
        dka[...] = jnp.zeros_like(dka)
        dva[...] = jnp.zeros_like(dva)

        def chunk(c, _):
            step = u * n_chunks + c
            slot = step % 2
            at = pl.ds(pl.multiple_of(c * CHUNK, CHUNK), CHUNK)

            @pl.when(step >= 2)
            def _():
                for a, st in enumerate((o_v, dq_v)):
                    pltpu.make_async_copy(st.at[slot], st.at[slot], out_send.at[a, slot]).wait()
            attend_chunk(c, q_v.at[:, at, :], do_v.at[:, at, :], k_v.at[0], v_v.at[0],
                         o_v.at[slot], dq_v.at[slot], dka, dva,
                         (kT, vT, qT, doT, sc_ref, dp_ref, oT, dqT, pb, sb), scale)
            for e in range(per_chunk):
                for a, (st, dst) in enumerate(((o_v, o), (dq_v, dq))):
                    place(st.at[slot, :, e * blk:(e + 1) * blk, :], dst.at[row, pl.ds(g * grp, grp)],
                          c * per_chunk + e, out_send.at[a, slot], out_recv.at[a])
            return 0
        lax.fori_loop(0, n_chunks, chunk, 0)

        @pl.when(u >= 1)
        def _():
            for a, st in enumerate((dk_v, dv_v)):
                pltpu.make_async_copy(st, st, g_send.at[a]).wait()
        dk_v[...] = (dka[...] * scale).astype(bf16)
        dv_v[...] = dva[...].astype(bf16)

        def spread(s, _):
            at = pl.ds(pl.multiple_of(s * blk, blk), blk)
            for a, (st, dst) in enumerate(((dk_v, dk), (dv_v, dv))):
                place(st.at[at, :], dst.at[row, g], s, g_send.at[a], out_recv.at[2 + a])
            return 0
        lax.fori_loop(0, n_dev, spread, 0)
        return 0
    lax.fori_loop(0, n_units, unit, 0)

    for a, st in enumerate((o_v, dq_v)):
        for slot in range(2):
            pltpu.make_async_copy(st.at[slot], st.at[slot], out_send.at[a, slot]).wait()
    for a, st in enumerate((dk_v, dv_v)):
        pltpu.make_async_copy(st, st, g_send.at[a]).wait()
    for a, (src, _, _) in enumerate(arrays):
        part = src.at[pl.ds(0, n_rows - own)]
        pltpu.make_async_copy(part, part, in_send.at[a]).wait()
    for a, dst in enumerate((o, dq, dk, dv)):
        part = dst.at[pl.ds(0, n_rows - own)]
        pltpu.make_async_copy(part, part, out_recv.at[a]).wait()


def solution(mesh):
    n_dev = mesh.shape['ctxo'] * mesh.shape['ctx']
    spec = P('data', CTX_AXES, None, None)

    def local_attn(q_in, k_in, v_in, do_in):
        n_rows, blk, n_heads, dim = q_in.shape
        n_kv = k_in.shape[2]
        grp = n_heads // n_kv
        seq = blk * n_dev
        n_units = n_rows // n_dev * n_kv
        n_chunks = seq // CHUNK
        to_heads = lambda x: jnp.swapaxes(x, 1, 2)
        any_spec = pl.BlockSpec(memory_space=pl.ANY)
        shape = jax.ShapeDtypeStruct
        q_shape = shape((n_rows, n_heads, blk, dim), bf16)
        k_shape = shape((n_rows, n_kv, blk, dim), bf16)
        got_q = shape((n_units, grp, seq, dim), bf16)
        got_k = shape((n_units, 1, seq, dim), bf16)
        vmem, dma = pltpu.VMEM, pltpu.SemaphoreType.DMA
        res = pl.pallas_call(
            functools.partial(kernel, n_dev),
            out_shape=(q_shape, q_shape, k_shape, k_shape, got_q, got_k, got_k, got_q),
            in_specs=[any_spec] * 4,
            out_specs=(any_spec,) * 8,
            scratch_shapes=[
                vmem((grp, seq, dim), bf16), vmem((grp, seq, dim), bf16),
                vmem((1, seq, dim), bf16), vmem((1, seq, dim), bf16),
                vmem((2, grp, CHUNK, dim), bf16), vmem((2, grp, CHUNK, dim), bf16),
                vmem((seq, dim), bf16), vmem((seq, dim), bf16),
                vmem((seq, dim), f32), vmem((seq, dim), f32),
                vmem((n_chunks, dim, CHUNK), bf16), vmem((n_chunks, dim, CHUNK), bf16),
                vmem((2, dim, CHUNK), bf16), vmem((2, dim, CHUNK), bf16),
                vmem((2, n_chunks, CHUNK, CHUNK), f32), vmem((n_chunks, CHUNK, CHUNK), f32),
                vmem((dim, CHUNK), f32), vmem((dim, CHUNK), f32),
                vmem((2, SUB, CHUNK), bf16), vmem((2, SUB, CHUNK), bf16),
                dma((4,)), dma((n_units, 4)), dma((2, 2)), dma((4,)), dma((4, n_dev)), dma((2,)),
            ],
            compiler_params=pltpu.CompilerParams(
                collective_id=0, has_side_effects=True, vmem_limit_bytes=63 * 2**20),
            name='rows_attention',
        )(*(to_heads(x) for x in (q_in, k_in, v_in, do_in)))
        return tuple(to_heads(x) for x in res[:4])

    return jax.shard_map(local_attn, mesh=mesh, in_specs=(spec,) * 4, out_specs=(spec,) * 4, check_vma=False)
```

time: 4970 us -> 732 us (0.15)
  waiting for transfers between devices: 3200 us -> 0 us
  matrix products: 1010 us -> 0 us
  Pallas kernels: 0 us -> 692 us
  local copies, waits for them, and re-layouts: 321 us -> 36.2 us
  other arithmetic: 221 us -> 0 us
  starting transfers between devices: 190 us -> 0 us
    ppermute x53 -> x0, waiting for transfers between devices: 3200 us -> none  [the longest x48 2990 us: send_next(): return lax.ppermute(tree_in, CTX_AXES, next_perm)]
    dot_general x34 -> x0, matrix products: 1010 us -> none  [the longest x5 211 us: pair_forward(): jnp.einsum('bhqgk,bkhd->bhqgd', prob_blk.astype(jnp.bfloat16), v_blk, pre...]
    pallas_call x0 -> x1, Pallas kernels: none -> 692 us  [local_attn(): pl.pallas_call(functools.partial(kernel, n_dev), out_shape=(q_shape, q_sh...]
    while x56 -> x0, local copies, waits for them, and re-layouts: 209 us -> none
    ppermute x53 -> x0, starting transfers between devices: 190 us -> none  [the longest x48 184 us: send_next(): return lax.ppermute(tree_in, CTX_AXES, next_perm)]
    while x15 -> x0, other arithmetic: 99.4 us -> none
    reduce_sum x5 -> x0, other arithmetic: 92.9 us -> none  [pair_forward(): row_sum = jnp.sum(prob_blk, axis=-1)]
    unnamed x41 -> x6, local copies, waits for them, and re-layouts: 112 us -> 29.1 us
  transfers between devices with their start and end apart: 53 -> 0, of which waited for: 28 -> 0; matrix products, arithmetic and copies ran while one was open for 20% -> 0% of each run, Pallas kernels for 0% -> 0%
where the time goes in v1:
time: 732 us; the launch traced here: 729 us
  Pallas kernels  692 us (95%)
  local copies, waits for them, and re-layouts  36.2 us (5%)
    pallas_call x1, Pallas kernels, local_attn(): pl.pallas_call(functools.partial(kernel, n_dev), out_shape=(q_shape, q_sh...  692 us
    unnamed x6, local copies, waits for them, and re-layouts  29.1 us

profile of v1, /device:TPU:5, one launch (start us, length us, event | category | flops | bytes accessed | tf_op | source)
XLA Modules:
  0.0 729.0 jit_solution(18297758249148545918)
XLA Ops:
  0.6 7.2 copy_bitcast_fusion
  7.8 692.1 %rows_attention.1 = (bf16[16,6,384,128]{3,2,1,0:T(8,128)(2,1)}, bf16[16,6,384,128]{3,2,1,0:T(8,128)(2,1)}, bf16[16,2,384,128]{3,2,1,0:T(8,128)(2,1)}, bf16[16,2,...) custom-call(bf16[16,6,384,128]{3,2,1,0:T(8,128)(2,1)} %bitcast.10, ...), custom_call_target="tpu_custom_call" | custom-call | tf_op jit(solution)/shard_map/rows_attention/pallas_call | solution.py:313
  699.9 0.0 copy-start
  699.9 7.0 copy.10
  706.8 0.0 copy-done
  706.9 4.9 copy.11
  711.8 8.6 %copy.16 = bf16[16,384,6,128]{3,1,2,0:T(8,128)(2,1)} copy(bf16[16,384,6,128]{3,1,2,0:T(8,128)(2,1)} %bitcast.13) | data formatting | bytes 18874368
  720.4 8.6 %copy.17 = bf16[16,384,6,128]{3,1,2,0:T(8,128)(2,1)} copy(bf16[16,384,6,128]{3,1,2,0:T(8,128)(2,1)} %bitcast.12) | data formatting | bytes 18874368
Async XLA Ops:
  699.9 7.0 copy-start

commit v2 on v1

v2 whole, which is shorter than its diff:
```python
import functools
import math
import jax
import jax.numpy as jnp
from jax import lax
from jax.experimental import pallas as pl
from jax.experimental.pallas import tpu as pltpu
from jax.sharding import PartitionSpec as P

CTX_AXES = ('ctxo', 'ctx')
MESH = pl.DeviceIdType.MESH
f32 = jnp.float32
bf16 = jnp.bfloat16
CHUNK = 768
SUB = 256
AHEAD = 3
LAG = 2


def dot(a, b):
    return jnp.dot(a, b, preferred_element_type=f32)


def fold(x, op):
    return op(x.reshape(x.shape[0] // 8, 8, x.shape[1]), axis=0)


def tile(i):
    return slice(i * SUB, (i + 1) * SUB)


def attend_chunk(c, q, do, kv, o, dq, g, s, scale, hooks):
    kT, vT, qT, doT, sc_ref, dp_ref, oT, dqT, pb, sb = s
    score_scale = scale * math.log2(math.e)
    n_sub = CHUNK // SUB
    n_heads = q.shape[0]

    def cols(ki, diag):
        return range(ki, n_sub) if diag else range(n_sub)

    lowest = tuple(jnp.full((8, SUB), -jnp.inf, f32) for _ in range(n_sub))

    def load_heads(h, b):
        for i in range(n_sub):
            qT[b, :, tile(i)] = q[h, tile(i), :].T
            doT[b, :, tile(i)] = do[h, tile(i), :].T

    def scores(j, b, m, ki, diag):
        for qi in cols(ki, diag):
            x = dot(kv[j, 0, tile(ki), :], qT[b, :, tile(qi)]) * score_scale
            if diag and ki == qi:
                key = lax.broadcasted_iota(jnp.int32, (SUB, SUB), 0)
                query = lax.broadcasted_iota(jnp.int32, (SUB, SUB), 1)
                x = jnp.where(key <= query, x, -jnp.inf)
            sc_ref[b, j, tile(ki), tile(qi)] = x
            m[qi] = jnp.maximum(m[qi], fold(x, jnp.max))

    def score_pass(b):
        def body(j, m, diag=False):
            m = list(m)
            for ki in range(n_sub):
                scores(j, b, m, ki, diag)
            return tuple(m)
        return body(c, lax.fori_loop(0, c, body, lowest), True)

    def forward_pass(b, m):
        top = [jnp.max(x, axis=0, keepdims=True) for x in m]
        oT[...] = jnp.zeros_like(oT)

        def body(j, l, diag=False):
            l, acc = list(l), [None] * n_sub

            def probs(ki):
                for qi in cols(ki, diag):
                    e = jnp.exp2(sc_ref[b, j, tile(ki), tile(qi)] - top[qi])
                    sc_ref[b, j, tile(ki), tile(qi)] = e
                    l[qi] = l[qi] + fold(e, jnp.sum)
                    pb[ki % 2, :, tile(qi)] = e.astype(bf16)

            def prob_grads(ki):
                for qi in cols(ki, diag):
                    dp_ref[j, tile(ki), tile(qi)] = dot(kv[j, 1, tile(ki), :], doT[b, :, tile(qi)])

            def outputs(ki):
                for qi in cols(ki, diag):
                    d = dot(vT[j, :, tile(ki)], pb[ki % 2, :, tile(qi)])
                    acc[qi] = d if acc[qi] is None else acc[qi] + d

            for ki in range(n_sub + 1):
                if ki < n_sub:
                    prob_grads(ki)
                    probs(ki)
                if ki:
                    outputs(ki - 1)
            for qi in range(n_sub):
                oT[:, tile(qi)] += acc[qi]
            return tuple(l)

        l = tuple(jnp.zeros((8, SUB), f32) for _ in range(n_sub))
        l = body(c, lax.fori_loop(0, c, body, l), True)
        return [1.0 / jnp.sum(x, axis=0, keepdims=True) for x in l]

    def finish_outputs(h, b, inv):
        drow = []
        for qi in range(n_sub):
            out = oT[:, tile(qi)] * inv[qi]
            drow.append(jnp.sum(out * doT[b, :, tile(qi)].astype(f32), axis=0, keepdims=True))
            o[h, tile(qi), :] = out.astype(bf16).T
        return drow

    def backward_pass(h, b, inv, drow, more):
        dqT[...] = jnp.zeros_like(dqT)

        def body(j, m, diag=False):
            m, acc = list(m), [None] * n_sub

            def score_grads(ki):
                for qi in cols(ki, diag):
                    p = sc_ref[b, j, tile(ki), tile(qi)] * inv[qi]
                    ds = p * (dp_ref[j, tile(ki), tile(qi)] - drow[qi])
                    pb[ki % 2, :, tile(qi)] = p.astype(bf16)
                    sb[ki % 2, :, tile(qi)] = ds.astype(bf16)

            def grads(ki):
                first = ki * SUB if diag else 0
                for qi in cols(ki, diag):
                    d = dot(kT[j, :, tile(ki)], sb[ki % 2, :, tile(qi)])
                    acc[qi] = d if acc[qi] is None else acc[qi] + d
                g[j, 1, tile(ki), :] += dot(pb[ki % 2, :, first:], do[h, first:, :])
                g[j, 0, tile(ki), :] += dot(sb[ki % 2, :, first:], q[h, first:, :])

            if more:
                scores(j, 1 - b, m, 0, diag)
            score_grads(0)
            for ki in range(1, n_sub):
                score_grads(ki)
                grads(ki - 1)
                if more:
                    scores(j, 1 - b, m, ki, diag)
            grads(n_sub - 1)
            for qi in range(n_sub):
                dqT[:, tile(qi)] += acc[qi]
            return tuple(m)

        m = body(c, lax.fori_loop(0, c, body, lowest), True)
        for qi in range(n_sub):
            dq[h, tile(qi), :] = (dqT[:, tile(qi)] * scale).astype(bf16).T
        return m

    load_heads(0, 0)
    m = score_pass(0)
    for h in range(n_heads):
        b = h % 2
        inv = forward_pass(b, m)
        drow = finish_outputs(h, b, inv)
        if h + 1 < n_heads:
            load_heads(h + 1, 1 - b)
        m = backward_pass(h, b, inv, drow, h + 1 < n_heads)
        if h < len(hooks):
            hooks[h]()


def kernel(q, k, v, do, o, dq, dk, dv, qd_l, kv_l, g_l,
           qd_v, kv_v, od_v, acc, g_in, g_out, kT, vT, *rest):
    scratch, sems = rest[:8], rest[8:]
    own_send, fed_send, kv_send, relay_send, qd_recv, kv_recv, g_send, g_recv, out_send, out_recv, grad_send, qd_load, kv_load, g_load = sems
    y, b = lax.axis_index('ctxo'), lax.axis_index('ctx')
    x, e = b // 2, b % 2
    n_rows, n_heads, blk, dim = q.shape
    n_kv = k.shape[1]
    grp = n_heads // n_kv
    lane_rows = n_rows // 2
    n_units = lane_rows
    c_own = 2 * y + x
    scale = 1.0 / math.sqrt(dim)

    def core(cy, cx, ce):
        return (0, cy, 2 * cx + ce)

    def both(kind, even, odd):
        return jnp.where(kind == 0, even, odd)

    def feeder(kind):
        return both(kind, 1 - y, y), both(kind, x, 1 - x)

    def partner(kind):
        return both(kind, y, 1 - y), both(kind, 1 - x, x)

    def chunk_of(kind, t):
        return both(kind, x + 2 * t, 2 * y + t)

    def row_of(w, lane):
        return lane * lane_rows + w

    def head_of(kind):
        return both(kind, y, x)

    def half(h):
        return pl.ds(pl.multiple_of(h * blk, blk), blk)

    def remote(src, dst, send, recv, dev):
        pltpu.make_async_remote_copy(src, dst, send, recv, device_id=dev, device_id_type=MESH).start()

    def drain(ref, sem):
        pltpu.make_async_copy(ref, ref, sem).wait()

    barrier = pltpu.get_barrier_semaphore()
    peers = [core(y, x, 1 - e)] + [core(1 - y, x, c) for c in range(2)] + [core(y, 1 - x, c) for c in range(2)]
    for dev in peers:
        pl.semaphore_signal(barrier, inc=1, device_id=dev, device_id_type=MESH)
    pl.semaphore_wait(barrier, len(peers))

    def first_has_kv(kind):
        return both(kind, x + y < 2, y == 0)

    def fed_goes_on(kind):
        return both(kind, (x == 0) | (y == 1), y == 0)

    def block(src, row, head, n):
        return src.at[row, pl.ds(head * n, n)]

    def send_ahead(w):
        kind = w % 2
        mine = head_of(kind)
        row = row_of(w, 1 - e)
        dev = core(y, x, 1 - e)
        for a, src in enumerate((q, do)):
            remote(block(src, row, mine, grp), qd_l.at[w, 0, a, :, half(e), :], own_send.at[a], qd_recv.at[w, 0], dev)
        for a, src in enumerate((k, v)):
            remote(src.at[row, mine], kv_l.at[w, c_own, a, half(e), :], own_send.at[2 + a], kv_recv.at[w, c_own], dev)
        fy, fx = feeder(kind)
        theirs = 1 - mine
        for lane in range(2):
            row = row_of(w, lane)
            dev = core(fy, fx, lane)
            for a, src in enumerate((k, v)):
                remote(src.at[row, theirs], kv_l.at[w, c_own, a, half(e), :], fed_send.at[2 + a], kv_recv.at[w, c_own], dev)
            for a, src in enumerate((q, do)):
                remote(block(src, row, theirs, grp), qd_l.at[w, 1, a, :, half(e), :], fed_send.at[a], qd_recv.at[w, 1], dev)
        py, px = partner(kind)

        @pl.when(first_has_kv(kind))
        def _():
            for lane in range(2):
                row = row_of(w, lane)
                for a, src in enumerate((k, v)):
                    remote(src.at[row, mine], kv_l.at[w, c_own, a, half(e), :], kv_send.at[a], kv_recv.at[w, c_own], core(py, px, lane))

    def fed_chunk(kind):
        fy, fx = feeder(kind)
        return 2 * fy + fx

    def pass_on(w):
        kind = w % 2
        c = fed_chunk(kind)
        drain(kv_l.at[w, c], kv_recv.at[w, c])
        py, px = partner(kind)

        @pl.when(fed_goes_on(kind))
        def _():
            remote(kv_l.at[w, c], kv_l.at[w, c], relay_send, kv_recv.at[w, c], core(py, px, e))

    def new_chunks(kind, t):
        return both(t, 0, chunk_of(kind, 0) + 1), chunk_of(kind, t) + 1

    def fetch(s):
        w, t = s // 2, s % 2
        kind, slot = w % 2, s % 2
        c = chunk_of(kind, t)
        own = c == c_own
        row, mine = row_of(w, e), head_of(kind)
        lo, hi = new_chunks(kind, t)

        def keys(j, _):
            dst = kv_v.at[w % 2, j]

            @pl.when(j == c_own)
            def _():
                other = kv_l.at[w, j, :, half(1 - e), :]
                drain(other, kv_recv.at[w, j])
                pltpu.make_async_copy(other, dst.at[:, half(1 - e), :], kv_load.at[w % 2, j]).start()
                for a, src in enumerate((k, v)):
                    pltpu.make_async_copy(src.at[row, mine], dst.at[a, half(e), :], kv_load.at[w % 2, j]).start()

            @pl.when(j != c_own)
            def _():
                @pl.when(j != fed_chunk(kind))
                def _():
                    drain(kv_l.at[w, j], kv_recv.at[w, j])
                pltpu.make_async_copy(kv_l.at[w, j], dst, kv_load.at[w % 2, j]).start()
            return 0
        lax.fori_loop(lo, hi, keys, 0)

        @pl.when(own)
        def _():
            other = qd_l.at[w, 0, :, :, half(1 - e), :]
            drain(other, qd_recv.at[w, 0])
            pltpu.make_async_copy(other, qd_v.at[slot, :, :, half(1 - e), :], qd_load.at[slot]).start()
            for a, src in enumerate((q, do)):
                pltpu.make_async_copy(block(src, row, mine, grp), qd_v.at[slot, a, :, half(e), :], qd_load.at[slot]).start()

        @pl.when(jnp.logical_not(own))
        def _():
            drain(qd_l.at[w, 1], qd_recv.at[w, 1])
            pltpu.make_async_copy(qd_l.at[w, 1], qd_v.at[slot], qd_load.at[slot]).start()

    def place(kind, c, send, pieces):
        fy, fx = feeder(kind)
        own = c == c_own
        oy, ox = jnp.where(own, y, fy), jnp.where(own, x, fx)
        for h in range(2):
            here = own & (e == h)
            for src, dst, recv in pieces(h):
                @pl.when(here)
                def _():
                    pltpu.make_async_copy(src, dst, send).start()

                @pl.when(jnp.logical_not(here))
                def _():
                    remote(src, dst, send, recv, core(oy, ox, h))

    def incoming(kind, a):
        return both(kind, (x == 0) | (a == 0), y == 0)

    def fetch_sums(w):
        kind = w % 2
        for a in range(2):
            @pl.when(incoming(kind, a))
            def _():
                drain(g_l.at[w, a], g_recv.at[w, a])
                pltpu.make_async_copy(g_l.at[w, a], g_in.at[a], g_load.at[a]).start()

    def merge(w):
        kind, slot = w % 2, w % (LAG + 1)
        row, mine = row_of(w, e), head_of(kind)
        for a in range(2):
            c = chunk_of(kind, a)

            @pl.when(w >= 1)
            def _():
                drain(g_out.at[a], grad_send.at[a])

            @pl.when(incoming(kind, a))
            def _():
                drain(g_in.at[a], g_load.at[a])
                g_out[a, 0] = ((acc[slot, c, 0] + g_in[a, 0]) * scale).astype(bf16)
                g_out[a, 1] = (acc[slot, c, 1] + g_in[a, 1]).astype(bf16)

            @pl.when(jnp.logical_not(incoming(kind, a)))
            def _():
                g_out[a, 0] = (acc[slot, c, 0] * scale).astype(bf16)
                g_out[a, 1] = acc[slot, c, 1].astype(bf16)
            place(kind, c, grad_send.at[a], lambda h: [
                (g_out.at[a, i, h * blk:(h + 1) * blk, :], dst.at[row, mine], out_recv.at[2 + i]) for i, dst in enumerate((dk, dv))])

    def n_sums_out(kind):
        return both(kind, 1 + x, 2 * y)

    def send_sums(w):
        kind, slot = w % 2, w % (LAG + 1)
        dev = core(*partner(kind), e)

        def one(c, a):
            remote(acc.at[slot, c], g_l.at[w, a], g_send.at[slot], g_recv.at[w, a], dev)

        @pl.when((kind == 0) & (x == 0))
        def _():
            one(1, 0)

        @pl.when((kind == 0) & (x == 1))
        def _():
            one(2, 1)
            one(0, 0)

        @pl.when((kind == 1) & (y == 1))
        def _():
            one(0, 0)
            one(1, 1)

    def sums_left(w):
        kind, slot = w % 2, w % (LAG + 1)
        n = n_sums_out(kind)
        for m in (1, 2):
            @pl.when(n == m)
            def _():
                drain(acc.at[slot, 0:m], g_send.at[slot])

    for w in range(AHEAD):
        send_ahead(w)
    pass_on(0)
    fetch(0)
    n_tasks = 2 * n_units

    def task(s, _):
        w, t = s // 2, s % 2
        kind, slot, a_slot = w % 2, s % 2, w % (LAG + 1)
        c = chunk_of(kind, t)

        @pl.when(t == 0)
        def _():
            @pl.when(w >= LAG + 1)
            def _():
                sums_left(w - LAG - 1)
            acc[a_slot] = jnp.zeros(acc.shape[1:], f32)
        lo, hi = new_chunks(kind, t)

        def turn(j, _):
            drain(kv_v.at[w % 2, j], kv_load.at[w % 2, j])
            kT[j] = kv_v[w % 2, j, 0].T
            vT[j] = kv_v[w % 2, j, 1].T
            return 0
        lax.fori_loop(lo, hi, turn, 0)
        drain(qd_v.at[slot], qd_load.at[slot])

        @pl.when(s >= 2)
        def _():
            drain(od_v.at[slot], out_send.at[slot])

        def early():
            @pl.when((t == 0) & (w + AHEAD < n_units))
            def _():
                send_ahead(w + AHEAD)

            @pl.when((t == 0) & (w + 1 < n_units))
            def _():
                pass_on(w + 1)

        def late():
            @pl.when(s + 1 < n_tasks)
            def _():
                fetch(s + 1)

            @pl.when((t == 1) & (w >= LAG))
            def _():
                fetch_sums(w - LAG)
        attend_chunk(c, qd_v.at[slot, 0], qd_v.at[slot, 1], kv_v.at[w % 2], od_v.at[slot, 0], od_v.at[slot, 1],
                     acc.at[a_slot], (kT, vT, *scratch), scale, (early, late))
        row, mine = row_of(w, e), head_of(kind)
        place(kind, c, out_send.at[slot], lambda h: [
            (od_v.at[slot, i, :, h * blk:(h + 1) * blk, :], block(dst, row, mine, grp), out_recv.at[i]) for i, dst in enumerate((o, dq))])

        @pl.when(t == 1)
        def _():
            send_sums(w)

            @pl.when(w >= LAG)
            def _():
                merge(w - LAG)
        return 0
    lax.fori_loop(0, n_tasks, task, 0)
    for w in range(n_units - LAG, n_units):
        fetch_sums(w)
        merge(w)

    for slot in range(2):
        drain(od_v.at[slot], out_send.at[slot])
        drain(g_out.at[slot], grad_send.at[slot])
    for w in range(n_units - LAG - 1, n_units):
        sums_left(w)
    part = n_units // 2
    for a, src in enumerate((q, do, k, v)):
        drain(src.at[0:part], own_send.at[a])
        drain(src.at[0:2 * part], fed_send.at[a])
    for kind in range(2):
        @pl.when(first_has_kv(kind))
        def _():
            for a, src in enumerate((k, v)):
                drain(src.at[0:part], kv_send.at[a])

        @pl.when(fed_goes_on(kind))
        def _():
            drain(kv_l.at[0:part, 0], relay_send)
    for a, dst in enumerate((o, dq, dk, dv)):
        drain(dst.at[0:3 * part], out_recv.at[a])


def solution(mesh):
    spec = P('data', CTX_AXES, None, None)

    def local_attn(q_in, k_in, v_in, do_in):
        n_rows, blk, n_heads, dim = q_in.shape
        n_kv = k_in.shape[2]
        grp = n_heads // n_kv
        n_units = n_rows // 2
        n_chunks = 4
        to_heads = lambda x: jnp.swapaxes(x, 1, 2)
        any_spec = pl.BlockSpec(memory_space=pl.ANY)
        shape = jax.ShapeDtypeStruct
        q_shape = shape((n_rows, n_heads, blk, dim), bf16)
        k_shape = shape((n_rows, n_kv, blk, dim), bf16)
        landing = (shape((n_units, 2, 2, grp, CHUNK, dim), bf16), shape((n_units, n_chunks, 2, CHUNK, dim), bf16),
                   shape((n_units, 2, 2, CHUNK, dim), f32))
        vmem, dma = pltpu.VMEM, pltpu.SemaphoreType.DMA
        res = pl.pallas_call(
            kernel,
            out_shape=(q_shape, q_shape, k_shape, k_shape, *landing),
            in_specs=[any_spec] * 4,
            out_specs=(any_spec,) * 7,
            scratch_shapes=[
                vmem((2, 2, grp, CHUNK, dim), bf16), vmem((2, n_chunks, 2, CHUNK, dim), bf16),
                vmem((2, 2, grp, CHUNK, dim), bf16),
                vmem((LAG + 1, n_chunks, 2, CHUNK, dim), f32),
                vmem((2, 2, CHUNK, dim), f32), vmem((2, 2, CHUNK, dim), bf16),
                vmem((n_chunks, dim, CHUNK), bf16), vmem((n_chunks, dim, CHUNK), bf16),
                vmem((2, dim, CHUNK), bf16), vmem((2, dim, CHUNK), bf16),
                vmem((2, n_chunks, CHUNK, CHUNK), f32), vmem((n_chunks, CHUNK, CHUNK), f32),
                vmem((dim, CHUNK), f32), vmem((dim, CHUNK), f32),
                vmem((2, SUB, CHUNK), bf16), vmem((2, SUB, CHUNK), bf16),
                dma((4,)), dma((4,)), dma((2,)), dma,
                dma((n_units, 2)), dma((n_units, n_chunks)),
                dma((LAG + 1,)), dma((n_units, 2)),
                dma((2,)), dma((4,)), dma((2,)), dma((2,)), dma((2, n_chunks)), dma((2,)),
            ],
            compiler_params=pltpu.CompilerParams(
                collective_id=0, has_side_effects=True, vmem_limit_bytes=63 * 2**20),
            name='pair_attention',
        )(*(to_heads(x) for x in (q_in, k_in, v_in, do_in)))
        return tuple(to_heads(x) for x in res[:4])

    return jax.shard_map(local_attn, mesh=mesh, in_specs=(spec,) * 4, out_specs=(spec,) * 4, check_vma=False)
```

time: 732 us -> 554 us (0.76)
  Pallas kernels: 692 us -> 517 us
    pallas_call x1, Pallas kernels: 692 us -> 517 us  [local_attn(): pl.pallas_call(kernel, out_shape=(q_shape, q_shape, k_shape, k_shape, *la...]
where the time goes in v2:
time: 554 us; the launch traced here: 553 us
  Pallas kernels  517 us (93%)
  local copies, waits for them, and re-layouts  36.2 us (7%)
    pallas_call x1, Pallas kernels, local_attn(): pl.pallas_call(kernel, out_shape=(q_shape, q_shape, k_shape, k_shape, *la...  517 us
    unnamed x6, local copies, waits for them, and re-layouts  29.1 us

profile of v2, /device:TPU:5, one launch (start us, length us, event | category | flops | bytes accessed | tf_op | source)
XLA Modules:
  0.0 553.5 jit_solution(7993777565775192182)
XLA Ops:
  0.6 7.2 %copy_bitcast_fusion = (bf16[16,2,384,128]{3,2,1,0:T(8,128)(2,1)}, bf16[16,2,384,128]{3,2,1,0:T(8,128)(2,1)}) fusion(bf16[16,384,2,128]{3,2,1,0:T(2,128)(2,1)} %param.6, bf16[16,384,2,128]{3,2,1,0:T(2,128)(2,1)} %param.5), kind=kLoop, calls=%fused_computation | loop fusion | bytes 12582912 | tf_op jit(solution)/shard_map/transpose | solution.py:486
  7.8 516.6 %pair_attention.1 = (bf16[16,6,384,128]{3,2,1,0:T(8,128)(2,1)}, bf16[16,6,384,128]{3,2,1,0:T(8,128)(2,1)}, bf16[16,2,384,128]{3,2,1,0:T(8,128)(2,1)}, bf16[16,2,...) custom-call(bf16[16,6,384,128]{3,2,1,0:T(8,128)(2,1)} %bitcast.10, ...), custom_call_target="tpu_custom_call" | custom-call | tf_op jit(solution)/shard_map/pair_attention/pallas_call | solution.py:494
  524.4 0.0 copy-start
  524.4 7.0 %copy.10 = bf16[16,384,2,128]{3,2,1,0:T(2,128)(2,1)} copy(bf16[16,384,2,128]{3,1,2,0:T(8,128)(2,1)} %bitcast.15) | data formatting | bytes 6291456
  531.3 0.0 copy-done
  531.4 4.9 copy.11
  536.3 8.6 %copy.16 = bf16[16,384,6,128]{3,1,2,0:T(8,128)(2,1)} copy(bf16[16,384,6,128]{3,1,2,0:T(8,128)(2,1)} %bitcast.13) | data formatting | bytes 18874368
  544.9 8.6 %copy.17 = bf16[16,384,6,128]{3,1,2,0:T(8,128)(2,1)} copy(bf16[16,384,6,128]{3,1,2,0:T(8,128)(2,1)} %bitcast.12) | data formatting | bytes 18874368
Async XLA Ops:
  524.4 7.0 %copy-start = (bf16[16,2,384,128]{3,2,1,0:T(8,128)(2,1)S(1)}, bf16[16,2,384,128]{3,2,1,0:T(8,128)(2,1)}, u32[]{:S(2)}) copy-start(bf16[16,2,384,128]{3,2,1,0:T(8,128)(2,1)} %get-tuple-element.11) | copy-start | bytes 9437188

commit v3 on v2

--- a/solution.py
+++ b/solution.py
@@ -13,8 +13,9 @@
 bf16 = jnp.bfloat16
 CHUNK = 768
 SUB = 256
-AHEAD = 3
+LEADS = ((20, 20), (5, 4), (8, 12), (4, 4), (4, 6))
 LAG = 2
+OUT_SLOTS = 4
 
 
 def dot(a, b):
@@ -180,6 +181,9 @@
     def both(kind, even, odd):
         return jnp.where(kind == 0, even, odd)
 
+    def kind_of(w):
+        return 1 - w % 2
+
     def feeder(kind):
         return both(kind, 1 - y, y), both(kind, x, 1 - x)
 
@@ -219,45 +223,48 @@
     def block(src, row, head, n):
         return src.at[row, pl.ds(head * n, n)]
 
-    def send_ahead(w):
-        kind = w % 2
-        mine = head_of(kind)
-        row = row_of(w, 1 - e)
-        dev = core(y, x, 1 - e)
+    def send_own(w, kind):
+        mine, row, dev = head_of(kind), row_of(w, 1 - e), core(y, x, 1 - e)
         for a, src in enumerate((q, do)):
             remote(block(src, row, mine, grp), qd_l.at[w, 0, a, :, half(e), :], own_send.at[a], qd_recv.at[w, 0], dev)
         for a, src in enumerate((k, v)):
             remote(src.at[row, mine], kv_l.at[w, c_own, a, half(e), :], own_send.at[2 + a], kv_recv.at[w, c_own], dev)
+
+    def feed_keys(w, kind):
         fy, fx = feeder(kind)
-        theirs = 1 - mine
         for lane in range(2):
-            row = row_of(w, lane)
-            dev = core(fy, fx, lane)
             for a, src in enumerate((k, v)):
-                remote(src.at[row, theirs], kv_l.at[w, c_own, a, half(e), :], fed_send.at[2 + a], kv_recv.at[w, c_own], dev)
+                remote(src.at[row_of(w, lane), 1 - head_of(kind)], kv_l.at[w, c_own, a, half(e), :],
+                       fed_send.at[2 + a], kv_recv.at[w, c_own], core(fy, fx, lane))
+
+    def feed_queries(w, kind):
+        fy, fx = feeder(kind)
+        for lane in range(2):
             for a, src in enumerate((q, do)):
-                remote(block(src, row, theirs, grp), qd_l.at[w, 1, a, :, half(e), :], fed_send.at[a], qd_recv.at[w, 1], dev)
+                remote(block(src, row_of(w, lane), 1 - head_of(kind), grp), qd_l.at[w, 1, a, :, half(e), :],
+                       fed_send.at[a], qd_recv.at[w, 1], core(fy, fx, lane))
+
+    def share_keys(w, kind):
         py, px = partner(kind)
 
         @pl.when(first_has_kv(kind))
         def _():
             for lane in range(2):
-                row = row_of(w, lane)
                 for a, src in enumerate((k, v)):
-                    remote(src.at[row, mine], kv_l.at[w, c_own, a, half(e), :], kv_send.at[a], kv_recv.at[w, c_own], core(py, px, lane))
+                    remote(src.at[row_of(w, lane), head_of(kind)], kv_l.at[w, c_own, a, half(e), :],
+                           kv_send.at[a], kv_recv.at[w, c_own], core(py, px, lane))
 
     def fed_chunk(kind):
         fy, fx = feeder(kind)
         return 2 * fy + fx
 
-    def pass_on(w):
-        kind = w % 2
+    def pass_on(w, kind):
         c = fed_chunk(kind)
-        drain(kv_l.at[w, c], kv_recv.at[w, c])
         py, px = partner(kind)
 
         @pl.when(fed_goes_on(kind))
         def _():
+            drain(kv_l.at[w, c], kv_recv.at[w, c])
             remote(kv_l.at[w, c], kv_l.at[w, c], relay_send, kv_recv.at[w, c], core(py, px, e))
 
     def new_chunks(kind, t):
@@ -265,7 +272,7 @@
 
     def fetch(s):
         w, t = s // 2, s % 2
-        kind, slot = w % 2, s % 2
+        kind, slot = kind_of(w), s % 2
         c = chunk_of(kind, t)
         own = c == c_own
         row, mine = row_of(w, e), head_of(kind)
@@ -284,7 +291,7 @@
 
             @pl.when(j != c_own)
             def _():
-                @pl.when(j != fed_chunk(kind))
+                @pl.when((j != fed_chunk(kind)) | jnp.logical_not(fed_goes_on(kind)))
                 def _():
                     drain(kv_l.at[w, j], kv_recv.at[w, j])
                 pltpu.make_async_copy(kv_l.at[w, j], dst, kv_load.at[w % 2, j]).start()
@@ -323,7 +330,7 @@
         return both(kind, (x == 0) | (a == 0), y == 0)
 
     def fetch_sums(w):
-        kind = w % 2
+        kind = kind_of(w)
         for a in range(2):
             @pl.when(incoming(kind, a))
             def _():
@@ -331,33 +338,33 @@
                 pltpu.make_async_copy(g_l.at[w, a], g_in.at[a], g_load.at[a]).start()
 
     def merge(w):
-        kind, slot = w % 2, w % (LAG + 1)
+        kind, slot = kind_of(w), w % (LAG + 1)
         row, mine = row_of(w, e), head_of(kind)
         for a in range(2):
             c = chunk_of(kind, a)
 
-            @pl.when(w >= 1)
-            def _():
-                drain(g_out.at[a], grad_send.at[a])
+            @pl.when(w >= 2)
+            def _():
+                drain(g_out.at[w % 2, a], grad_send.at[w % 2, a])
 
             @pl.when(incoming(kind, a))
             def _():
                 drain(g_in.at[a], g_load.at[a])
-                g_out[a, 0] = ((acc[slot, c, 0] + g_in[a, 0]) * scale).astype(bf16)
-                g_out[a, 1] = (acc[slot, c, 1] + g_in[a, 1]).astype(bf16)
+                g_out[w % 2, a, 0] = ((acc[slot, c, 0] + g_in[a, 0]) * scale).astype(bf16)
+                g_out[w % 2, a, 1] = (acc[slot, c, 1] + g_in[a, 1]).astype(bf16)
 
             @pl.when(jnp.logical_not(incoming(kind, a)))
             def _():
-                g_out[a, 0] = (acc[slot, c, 0] * scale).astype(bf16)
-                g_out[a, 1] = acc[slot, c, 1].astype(bf16)
-            place(kind, c, grad_send.at[a], lambda h: [
-                (g_out.at[a, i, h * blk:(h + 1) * blk, :], dst.at[row, mine], out_recv.at[2 + i]) for i, dst in enumerate((dk, dv))])
+                g_out[w % 2, a, 0] = (acc[slot, c, 0] * scale).astype(bf16)
+                g_out[w % 2, a, 1] = acc[slot, c, 1].astype(bf16)
+            place(kind, c, grad_send.at[w % 2, a], lambda h: [
+                (g_out.at[w % 2, a, i, h * blk:(h + 1) * blk, :], dst.at[row, mine], out_recv.at[2 + i]) for i, dst in enumerate((dk, dv))])
 
     def n_sums_out(kind):
         return both(kind, 1 + x, 2 * y)
 
     def send_sums(w):
-        kind, slot = w % 2, w % (LAG + 1)
+        kind, slot = kind_of(w), w % (LAG + 1)
         dev = core(*partner(kind), e)
 
         def one(c, a):
@@ -378,22 +385,35 @@
             one(1, 1)
 
     def sums_left(w):
-        kind, slot = w % 2, w % (LAG + 1)
+        kind, slot = kind_of(w), w % (LAG + 1)
         n = n_sums_out(kind)
         for m in (1, 2):
             @pl.when(n == m)
             def _():
                 drain(acc.at[slot, 0:m], g_send.at[slot])
 
-    for w in range(AHEAD):
-        send_ahead(w)
-    pass_on(0)
+    jobs = (send_own, share_keys, feed_keys, pass_on, feed_queries)
+
+    def run_due(h):
+        for job, leads in zip(jobs, LEADS):
+            for kind in range(2):
+                later = h + leads[kind]
+                w = later // 4
+
+                @pl.when((later % 4 == 0) & (w < n_units) & (kind_of(w) == kind))
+                def _():
+                    job(w, kind)
+
+    first = [(4 * w - LEADS[j][kind_of(w)], w, j) for w in range(n_units) for j in range(len(jobs))]
+    for h, w, j in sorted(first):
+        if h < 0:
+            jobs[j](w, kind_of(w))
     fetch(0)
     n_tasks = 2 * n_units
 
     def task(s, _):
         w, t = s // 2, s % 2
-        kind, slot, a_slot = w % 2, s % 2, w % (LAG + 1)
+        kind, slot, a_slot = kind_of(w), s % 2, w % (LAG + 1)
         c = chunk_of(kind, t)
 
         @pl.when(t == 0)
@@ -412,20 +432,18 @@
         lax.fori_loop(lo, hi, turn, 0)
         drain(qd_v.at[slot], qd_load.at[slot])
 
-        @pl.when(s >= 2)
-        def _():
-            drain(od_v.at[slot], out_send.at[slot])
+        o_slot = s % OUT_SLOTS
+
+        @pl.when(s >= OUT_SLOTS)
+        def _():
+            drain(od_v.at[o_slot], out_send.at[o_slot])
 
         def early():
-            @pl.when((t == 0) & (w + AHEAD < n_units))
-            def _():
-                send_ahead(w + AHEAD)
-
-            @pl.when((t == 0) & (w + 1 < n_units))
-            def _():
-                pass_on(w + 1)
+            run_due(2 * s)
 
         def late():
+            run_due(2 * s + 1)
+
             @pl.when(s + 1 < n_tasks)
             def _():
                 fetch(s + 1)
@@ -433,11 +451,11 @@
             @pl.when((t == 1) & (w >= LAG))
             def _():
                 fetch_sums(w - LAG)
-        attend_chunk(c, qd_v.at[slot, 0], qd_v.at[slot, 1], kv_v.at[w % 2], od_v.at[slot, 0], od_v.at[slot, 1],
+        attend_chunk(c, qd_v.at[slot, 0], qd_v.at[slot, 1], kv_v.at[w % 2], od_v.at[o_slot, 0], od_v.at[o_slot, 1],
                      acc.at[a_slot], (kT, vT, *scratch), scale, (early, late))
         row, mine = row_of(w, e), head_of(kind)
-        place(kind, c, out_send.at[slot], lambda h: [
-            (od_v.at[slot, i, :, h * blk:(h + 1) * blk, :], block(dst, row, mine, grp), out_recv.at[i]) for i, dst in enumerate((o, dq))])
+        place(kind, c, out_send.at[o_slot], lambda h: [
+            (od_v.at[o_slot, i, :, h * blk:(h + 1) * blk, :], block(dst, row, mine, grp), out_recv.at[i]) for i, dst in enumerate((o, dq))])
 
         @pl.when(t == 1)
         def _():
@@ -452,9 +470,11 @@
         fetch_sums(w)
         merge(w)
 
+    for slot in range(OUT_SLOTS):
+        drain(od_v.at[slot], out_send.at[slot])
     for slot in range(2):
-        drain(od_v.at[slot], out_send.at[slot])
-        drain(g_out.at[slot], grad_send.at[slot])
+        for a in range(2):
+            drain(g_out.at[slot, a], grad_send.at[slot, a])
     for w in range(n_units - LAG - 1, n_units):
         sums_left(w)
     part = n_units // 2
@@ -498,9 +518,9 @@
             out_specs=(any_spec,) * 7,
             scratch_shapes=[
                 vmem((2, 2, grp, CHUNK, dim), bf16), vmem((2, n_chunks, 2, CHUNK, dim), bf16),
-                vmem((2, 2, grp, CHUNK, dim), bf16),
+                vmem((OUT_SLOTS, 2, grp, CHUNK, dim), bf16),
                 vmem((LAG + 1, n_chunks, 2, CHUNK, dim), f32),
-                vmem((2, 2, CHUNK, dim), f32), vmem((2, 2, CHUNK, dim), bf16),
+                vmem((2, 2, CHUNK, dim), f32), vmem((2, 2, 2, CHUNK, dim), bf16),
                 vmem((n_chunks, dim, CHUNK), bf16), vmem((n_chunks, dim, CHUNK), bf16),
                 vmem((2, dim, CHUNK), bf16), vmem((2, dim, CHUNK), bf16),
                 vmem((2, n_chunks, CHUNK, CHUNK), f32), vmem((n_chunks, CHUNK, CHUNK), f32),
@@ -509,7 +529,7 @@
                 dma((4,)), dma((4,)), dma((2,)), dma,
                 dma((n_units, 2)), dma((n_units, n_chunks)),
                 dma((LAG + 1,)), dma((n_units, 2)),
-                dma((2,)), dma((4,)), dma((2,)), dma((2,)), dma((2, n_chunks)), dma((2,)),
+                dma((OUT_SLOTS,)), dma((4,)), dma((2, 2)), dma((2,)), dma((2, n_chunks)), dma((2,)),
             ],
             compiler_params=pltpu.CompilerParams(
                 collective_id=0, has_side_effects=True, vmem_limit_bytes=63 * 2**20),

time: 554 us -> 483 us (0.87)
  Pallas kernels: 517 us -> 446 us
    pallas_call x1, Pallas kernels: 517 us -> 446 us  [local_attn(): pl.pallas_call(kernel, out_shape=(q_shape, q_shape, k_shape, k_shape, *la...]
where the time goes in v3:
time: 483 us; the launch traced here: 482 us
  Pallas kernels  446 us (92%)
  local copies, waits for them, and re-layouts  36.2 us (7%)
    pallas_call x1, Pallas kernels, local_attn(): pl.pallas_call(kernel, out_shape=(q_shape, q_shape, k_shape, k_shape, *la...  446 us
    unnamed x6, local copies, waits for them, and re-layouts  29.1 us

profile of v3, /device:TPU:5, one launch (start us, length us, event | category | flops | bytes accessed | tf_op | source)
XLA Modules:
  0.0 482.4 jit_solution(7323705067869335519)
XLA Ops:
  0.6 7.2 %copy_bitcast_fusion = (bf16[16,2,384,128]{3,2,1,0:T(8,128)(2,1)}, bf16[16,2,384,128]{3,2,1,0:T(8,128)(2,1)}) fusion(bf16[16,384,2,128]{3,2,1,0:T(2,128)(2,1)} %param.6, bf16[16,384,2,128]{3,2,1,0:T(2,128)(2,1)} %param.5), kind=kLoop, calls=%fused_computation | loop fusion | bytes 12582912 | tf_op jit(solution)/shard_map/transpose | solution.py:506
  7.8 445.5 %pair_attention.1 = (bf16[16,6,384,128]{3,2,1,0:T(8,128)(2,1)}, bf16[16,6,384,128]{3,2,1,0:T(8,128)(2,1)}, bf16[16,2,384,128]{3,2,1,0:T(8,128)(2,1)}, bf16[16,2,...) custom-call(bf16[16,6,384,128]{3,2,1,0:T(8,128)(2,1)} %bitcast.10, ...), custom_call_target="tpu_custom_call" | custom-call | tf_op jit(solution)/shard_map/pair_attention/pallas_call | solution.py:514
  453.4 0.0 copy-start
  453.4 7.0 %copy.10 = bf16[16,384,2,128]{3,2,1,0:T(2,128)(2,1)} copy(bf16[16,384,2,128]{3,1,2,0:T(8,128)(2,1)} %bitcast.15) | data formatting | bytes 6291456
  460.3 0.0 copy-done
  460.3 4.9 %copy.11 = bf16[16,384,2,128]{3,2,1,0:T(2,128)(2,1)} copy(bf16[16,384,2,128]{3,1,2,0:T(8,128)(2,1)S(1)} %bitcast.14) | data formatting | bytes 6291456
  465.2 8.6 %copy.16 = bf16[16,384,6,128]{3,1,2,0:T(8,128)(2,1)} copy(bf16[16,384,6,128]{3,1,2,0:T(8,128)(2,1)} %bitcast.13) | data formatting | bytes 18874368
  473.8 8.6 %copy.17 = bf16[16,384,6,128]{3,1,2,0:T(8,128)(2,1)} copy(bf16[16,384,6,128]{3,1,2,0:T(8,128)(2,1)} %bitcast.12) | data formatting | bytes 18874368
Async XLA Ops:
  453.4 7.0 %copy-start = (bf16[16,2,384,128]{3,2,1,0:T(8,128)(2,1)S(1)}, bf16[16,2,384,128]{3,2,1,0:T(8,128)(2,1)}, u32[]{:S(2)}) copy-start(bf16[16,2,384,128]{3,2,1,0:T(8,128)(2,1)} %get-tuple-element.11) | copy-start | bytes 9437188

commit v4 on v3

--- a/solution.py
+++ b/solution.py
@@ -13,7 +13,8 @@
 bf16 = jnp.bfloat16
 CHUNK = 768
 SUB = 256
-LEADS = ((20, 20), (5, 4), (8, 12), (4, 4), (4, 6))
+LEADS = (20, 10, 14, 6, 10)
+KIND_1 = ((1, 3, 7), (0, 3, 4, 6))
 LAG = 2
 OUT_SLOTS = 4
 
@@ -181,8 +182,8 @@
     def both(kind, even, odd):
         return jnp.where(kind == 0, even, odd)
 
-    def kind_of(w):
-        return 1 - w % 2
+    def kind_of(w, lane):
+        return sum(jnp.where((lane == c) & (w == i), 1, 0) for c in range(2) for i in KIND_1[c])
 
     def feeder(kind):
         return both(kind, 1 - y, y), both(kind, x, 1 - x)
@@ -223,56 +224,48 @@
     def block(src, row, head, n):
         return src.at[row, pl.ds(head * n, n)]
 
-    def send_own(w, kind):
-        mine, row, dev = head_of(kind), row_of(w, 1 - e), core(y, x, 1 - e)
+    def send_own(w, lane, kind):
+        mine, row, dev = head_of(kind), row_of(w, lane), core(y, x, lane)
         for a, src in enumerate((q, do)):
             remote(block(src, row, mine, grp), qd_l.at[w, 0, a, :, half(e), :], own_send.at[a], qd_recv.at[w, 0], dev)
         for a, src in enumerate((k, v)):
             remote(src.at[row, mine], kv_l.at[w, c_own, a, half(e), :], own_send.at[2 + a], kv_recv.at[w, c_own], dev)
 
-    def feed_keys(w, kind):
-        fy, fx = feeder(kind)
-        for lane in range(2):
+    def feed_keys(w, lane, kind):
+        for a, src in enumerate((k, v)):
+            remote(src.at[row_of(w, lane), 1 - head_of(kind)], kv_l.at[w, c_own, a, half(e), :],
+                   fed_send.at[2 + a], kv_recv.at[w, c_own], core(*feeder(kind), lane))
+
+    def feed_queries(w, lane, kind):
+        for a, src in enumerate((q, do)):
+            remote(block(src, row_of(w, lane), 1 - head_of(kind), grp), qd_l.at[w, 1, a, :, half(e), :],
+                   fed_send.at[a], qd_recv.at[w, 1], core(*feeder(kind), lane))
+
+    def share_keys(w, lane, kind):
+        @pl.when(first_has_kv(kind))
+        def _():
             for a, src in enumerate((k, v)):
-                remote(src.at[row_of(w, lane), 1 - head_of(kind)], kv_l.at[w, c_own, a, half(e), :],
-                       fed_send.at[2 + a], kv_recv.at[w, c_own], core(fy, fx, lane))
-
-    def feed_queries(w, kind):
-        fy, fx = feeder(kind)
-        for lane in range(2):
-            for a, src in enumerate((q, do)):
-                remote(block(src, row_of(w, lane), 1 - head_of(kind), grp), qd_l.at[w, 1, a, :, half(e), :],
-                       fed_send.at[a], qd_recv.at[w, 1], core(fy, fx, lane))
-
-    def share_keys(w, kind):
-        py, px = partner(kind)
-
-        @pl.when(first_has_kv(kind))
-        def _():
-            for lane in range(2):
-                for a, src in enumerate((k, v)):
-                    remote(src.at[row_of(w, lane), head_of(kind)], kv_l.at[w, c_own, a, half(e), :],
-                           kv_send.at[a], kv_recv.at[w, c_own], core(py, px, lane))
+                remote(src.at[row_of(w, lane), head_of(kind)], kv_l.at[w, c_own, a, half(e), :],
+                       kv_send.at[a], kv_recv.at[w, c_own], core(*partner(kind), lane))
 
     def fed_chunk(kind):
         fy, fx = feeder(kind)
         return 2 * fy + fx
 
-    def pass_on(w, kind):
+    def pass_on(w, lane, kind):
         c = fed_chunk(kind)
-        py, px = partner(kind)
 
         @pl.when(fed_goes_on(kind))
         def _():
             drain(kv_l.at[w, c], kv_recv.at[w, c])
-            remote(kv_l.at[w, c], kv_l.at[w, c], relay_send, kv_recv.at[w, c], core(py, px, e))
+            remote(kv_l.at[w, c], kv_l.at[w, c], relay_send, kv_recv.at[w, c], core(*partner(kind), lane))
 
     def new_chunks(kind, t):
         return both(t, 0, chunk_of(kind, 0) + 1), chunk_of(kind, t) + 1
 
     def fetch(s):
         w, t = s // 2, s % 2
-        kind, slot = kind_of(w), s % 2
+        kind, slot = kind_of(w, e), s % 2
         c = chunk_of(kind, t)
         own = c == c_own
         row, mine = row_of(w, e), head_of(kind)
@@ -330,7 +323,7 @@
         return both(kind, (x == 0) | (a == 0), y == 0)
 
     def fetch_sums(w):
-        kind = kind_of(w)
+        kind = kind_of(w, e)
         for a in range(2):
             @pl.when(incoming(kind, a))
             def _():
@@ -338,7 +331,7 @@
                 pltpu.make_async_copy(g_l.at[w, a], g_in.at[a], g_load.at[a]).start()
 
     def merge(w):
-        kind, slot = kind_of(w), w % (LAG + 1)
+        kind, slot = kind_of(w, e), w % (LAG + 1)
         row, mine = row_of(w, e), head_of(kind)
         for a in range(2):
             c = chunk_of(kind, a)
@@ -364,7 +357,7 @@
         return both(kind, 1 + x, 2 * y)
 
     def send_sums(w):
-        kind, slot = kind_of(w), w % (LAG + 1)
+        kind, slot = kind_of(w, e), w % (LAG + 1)
         dev = core(*partner(kind), e)
 
         def one(c, a):
@@ -385,35 +378,37 @@
             one(1, 1)
 
     def sums_left(w):
-        kind, slot = kind_of(w), w % (LAG + 1)
+        kind, slot = kind_of(w, e), w % (LAG + 1)
         n = n_sums_out(kind)
         for m in (1, 2):
             @pl.when(n == m)
             def _():
                 drain(acc.at[slot, 0:m], g_send.at[slot])
 
-    jobs = (send_own, share_keys, feed_keys, pass_on, feed_queries)
+    jobs = ((send_own, (1 - e,)), (share_keys, (0, 1)), (feed_keys, (0, 1)), (pass_on, (e,)), (feed_queries, (0, 1)))
 
     def run_due(h):
-        for job, leads in zip(jobs, LEADS):
-            for kind in range(2):
-                later = h + leads[kind]
-                w = later // 4
-
-                @pl.when((later % 4 == 0) & (w < n_units) & (kind_of(w) == kind))
-                def _():
-                    job(w, kind)
-
-    first = [(4 * w - LEADS[j][kind_of(w)], w, j) for w in range(n_units) for j in range(len(jobs))]
+        for (job, lanes), lead in zip(jobs, LEADS):
+            later = h + lead
+            w = later // 4
+
+            @pl.when((later % 4 == 0) & (w < n_units))
+            def _():
+                for lane in lanes:
+                    job(w, lane, kind_of(w, lane))
+
+    first = [(4 * w - LEADS[j], w, j) for w in range(n_units) for j in range(len(jobs))]
     for h, w, j in sorted(first):
         if h < 0:
-            jobs[j](w, kind_of(w))
+            job, lanes = jobs[j]
+            for lane in lanes:
+                job(w, lane, kind_of(w, lane))
     fetch(0)
     n_tasks = 2 * n_units
 
     def task(s, _):
         w, t = s // 2, s % 2
-        kind, slot, a_slot = kind_of(w), s % 2, w % (LAG + 1)
+        kind, slot, a_slot = kind_of(w, e), s % 2, w % (LAG + 1)
         c = chunk_of(kind, t)
 
         @pl.when(t == 0)
@@ -481,17 +476,71 @@
     for a, src in enumerate((q, do, k, v)):
         drain(src.at[0:part], own_send.at[a])
         drain(src.at[0:2 * part], fed_send.at[a])
+    n_odd = [len(units) for units in KIND_1]
     for kind in range(2):
+        n_kind = [n if kind else n_units - n for n in n_odd]
+
         @pl.when(first_has_kv(kind))
         def _():
             for a, src in enumerate((k, v)):
-                drain(src.at[0:part], kv_send.at[a])
-
-        @pl.when(fed_goes_on(kind))
-        def _():
-            drain(kv_l.at[0:part, 0], relay_send)
+                drain(src.at[0:sum(n_kind), 0], kv_send.at[a])
+
+        for lane in range(2):
+            @pl.when(fed_goes_on(kind) & (e == lane))
+            def _():
+                drain(kv_l.at[0:n_kind[lane], 0], relay_send)
     for a, dst in enumerate((o, dq, dk, dv)):
         drain(dst.at[0:3 * part], out_recv.at[a])
+
+
+def finish_kernel(o, dq, dk, dv, o_out, dq_out, dk_out, dv_out, ring, g_in, g_out, ring_in, ring_out, g_load, g_store):
+    n_rows, n_kv, blk, _ = dk.shape
+    half = SUB // n_kv
+    at = lax.broadcasted_iota(jnp.int32, (SUB, SUB), 0)
+    take = lax.broadcasted_iota(jnp.int32, (SUB, SUB), 1)
+    perm = jnp.where(take == (at % n_kv) * half + at // n_kv, 1.0, 0.0).astype(bf16)
+    pairs = ((o, o_out), (dq, dq_out))
+    grads = ((dk, dk_out), (dv, dv_out))
+
+    def move(i, out):
+        src, dst = pairs[i % 2]
+        if out:
+            return pltpu.make_async_copy(ring.at[i], dst.at[i // 2], ring_out.at[i])
+        return pltpu.make_async_copy(src.at[i // 2], ring.at[i], ring_in.at[i])
+
+    def grad_rows(r):
+        return pl.ds(4 * (r // 4), 4)
+
+    def load(a, r):
+        return pltpu.make_async_copy(grads[a][0].at[grad_rows(r)], g_in.at[a, grad_rows(r)], g_load.at[a, r // 4])
+
+    def store(a, r):
+        return pltpu.make_async_copy(g_out.at[a, grad_rows(r)], grads[a][1].at[grad_rows(r)], g_store.at[a, r // 4])
+
+    n = 2 * n_rows
+    for i in range(4):
+        move(i, False).start()
+    for r in range(0, n_rows, 4):
+        load(0, r).start()
+        load(1, r).start()
+    for i in range(4, n):
+        move(i, False).start()
+    for i in range(n):
+        move(i, False).wait()
+        move(i, True).start()
+        a, r = i % 2, i // 2
+        if r % 4 == 0:
+            load(a, r).wait()
+        for p in range(blk // half):
+            x = jnp.concatenate([g_in[a, r, h, p * half:(p + 1) * half, :] for h in range(n_kv)], 0)
+            g_out[a, r, p * SUB:(p + 1) * SUB, :] = dot(perm, x).astype(bf16)
+        if r % 4 == 3:
+            store(a, r).start()
+    for i in range(n):
+        move(i, True).wait()
+    for r in range(0, n_rows, 4):
+        store(0, r).wait()
+        store(1, r).wait()
 
 
 def solution(mesh):
@@ -535,6 +584,20 @@
                 collective_id=0, has_side_effects=True, vmem_limit_bytes=63 * 2**20),
             name='pair_attention',
         )(*(to_heads(x) for x in (q_in, k_in, v_in, do_in)))
-        return tuple(to_heads(x) for x in res[:4])
+        joined = shape((n_rows, blk * n_kv, dim), bf16)
+        o, dq, dk, dv = pl.pallas_call(
+            finish_kernel,
+            out_shape=(q_shape, q_shape, joined, joined),
+            in_specs=[any_spec] * 4,
+            out_specs=(any_spec,) * 4,
+            scratch_shapes=[
+                vmem((2 * n_rows, n_heads, blk, dim), bf16),
+                vmem((2, n_rows, n_kv, blk, dim), bf16), vmem((2, n_rows, n_kv * blk, dim), bf16),
+                dma((2 * n_rows,)), dma((2 * n_rows,)), dma((2, n_rows // 4)), dma((2, n_rows // 4)),
+            ],
+            compiler_params=pltpu.CompilerParams(vmem_limit_bytes=62 * 2**20),
+            name='finish',
+        )(*res[:4])
+        return to_heads(o), to_heads(dq), dk.reshape(k_in.shape), dv.reshape(k_in.shape)
 
     return jax.shard_map(local_attn, mesh=mesh, in_specs=(spec,) * 4, out_specs=(spec,) * 4, check_vma=False)

time: 483 us -> 460 us (0.952)
  local copies, waits for them, and re-layouts: 36.2 us -> 7.18 us
  Pallas kernels: 446 us -> 452 us
    unnamed x6 -> x0, local copies, waits for them, and re-layouts: 29.1 us -> none
    pallas_call x0 -> x1, Pallas kernels: none -> 16.4 us  [local_attn(): pl.pallas_call(finish_kernel, out_shape=(q_shape, q_shape, joined, joined...]
    pallas_call x1, Pallas kernels: 446 us -> 435 us  [local_attn(): pl.pallas_call(kernel, out_shape=(q_shape, q_shape, k_shape, k_shape, *la...]
where the time goes in v4:
time: 460 us
  Pallas kernels  452 us (98%)
  local copies, waits for them, and re-layouts  7.18 us (2%)
    pallas_call x1, Pallas kernels, local_attn(): pl.pallas_call(kernel, out_shape=(q_shape, q_shape, k_shape, k_shape, *la...  435 us
    pallas_call x1, Pallas kernels, local_attn(): pl.pallas_call(finish_kernel, out_shape=(q_shape, q_shape, joined, joined...  16.4 us

profile of v4, /device:TPU:5, one launch (start us, length us, event | category | flops | bytes accessed | tf_op | source)
XLA Modules:
  0.0 459.5 jit_solution(198365555666163593)
XLA Ops:
  0.6 7.2 %copy_bitcast_fusion = (bf16[16,2,384,128]{3,2,1,0:T(8,128)(2,1)}, bf16[16,2,384,128]{3,2,1,0:T(8,128)(2,1)}) fusion(bf16[16,384,2,128]{3,2,1,0:T(2,128)(2,1)} %param.6, bf16[16,384,2,128]{3,2,1,0:T(2,128)(2,1)} %param.5), kind=kLoop, calls=%fused_computation | loop fusion | bytes 12582912 | tf_op jit(solution)/shard_map/transpose | solution.py:555
  7.8 435.1 %pair_attention.1 = (bf16[16,6,384,128]{3,2,1,0:T(8,128)(2,1)}, bf16[16,6,384,128]{3,2,1,0:T(8,128)(2,1)}, bf16[16,2,384,128]{3,2,1,0:T(8,128)(2,1)}, bf16[16,2,...) custom-call(bf16[16,6,384,128]{3,2,1,0:T(8,128)(2,1)} %bitcast.10, ...), custom_call_target="tpu_custom_call" | custom-call | tf_op jit(solution)/shard_map/pair_attention/pallas_call | solution.py:563
  442.9 16.4 %finish.1 = (bf16[16,6,384,128]{3,2,1,0:T(8,128)(2,1)}, bf16[16,6,384,128]{3,2,1,0:T(8,128)(2,1)}, bf16[16,768,128]{2,1,0:T(8,128)(2,1)}, bf16[16,768,128]{2,1,0:T(8,128)(2,1)}) custom-call(bf16[16,6,384,128]{3,2,1,0:T(8,128)(2,1)} %get-tuple-element.12.o, bf16[16,6,384,128]{3,2,1,0:T(8,128)(2,1)} %get-tuple-element.13.dq, ...), custom_call_target="tpu_custom_call" | custom-call | tf_op jit(solution)/shard_map/finish/pallas_call | solution.py:588

commit v5 on v4

--- a/solution.py
+++ b/solution.py
@@ -162,14 +162,14 @@
             hooks[h]()
 
 
-def kernel(q, k, v, do, o, dq, dk, dv, qd_l, kv_l, g_l,
+def kernel(q, k_raw, v_raw, do, o, dq, dk, dv, k, v, qd_l, kv_l, g_l,
            qd_v, kv_v, od_v, acc, g_in, g_out, kT, vT, *rest):
     scratch, sems = rest[:8], rest[8:]
     own_send, fed_send, kv_send, relay_send, qd_recv, kv_recv, g_send, g_recv, out_send, out_recv, grad_send, qd_load, kv_load, g_load = sems
     y, b = lax.axis_index('ctxo'), lax.axis_index('ctx')
     x, e = b // 2, b % 2
     n_rows, n_heads, blk, dim = q.shape
-    n_kv = k.shape[1]
+    n_kv = k.shape[1] // blk
     grp = n_heads // n_kv
     lane_rows = n_rows // 2
     n_units = lane_rows
@@ -224,16 +224,45 @@
     def block(src, row, head, n):
         return src.at[row, pl.ds(head * n, n)]
 
+    def split_heads():
+        part = SUB // n_kv
+        at = lax.broadcasted_iota(jnp.int32, (SUB, SUB), 0)
+        take = lax.broadcasted_iota(jnp.int32, (SUB, SUB), 1)
+        perm = jnp.where(take == (at % part) * n_kv + at // part, 1.0, 0.0).astype(bf16)
+
+        def room(a, r):
+            return od_v.at[r // 6, r // 3 % 2, r % 3] if a else kv_v.at[r // 8, r // 2 % 4, r % 2]
+
+        for a, raw in enumerate((k_raw, v_raw)):
+            for r in range(n_rows):
+                pltpu.make_async_copy(raw.at[r], room(a, r), kv_load.at[a, r // 4]).start()
+        for a, (raw, dst) in enumerate(((k_raw, k), (v_raw, v))):
+            def sort(r, _):
+                @pl.when(r % 4 == 0)
+                def _():
+                    drain(raw.at[0:4], kv_load.at[a, r // 4])
+                x = room(a, r)
+                y = [dot(perm, x[tile(p), :]).astype(bf16) for p in range(n_kv * blk // SUB)]
+                for p, rows in enumerate(y):
+                    for h in range(n_kv):
+                        x[h * blk + p * part:h * blk + (p + 1) * part, :] = rows[h * part:(h + 1) * part]
+                return 0
+            lax.fori_loop(0, n_rows, sort, 0)
+            for r in range(n_rows):
+                pltpu.make_async_copy(room(a, r), dst.at[r], qd_load.at[a]).start()
+        for a, dst in enumerate((k, v)):
+            drain(dst, qd_load.at[a])
+
     def send_own(w, lane, kind):
         mine, row, dev = head_of(kind), row_of(w, lane), core(y, x, lane)
         for a, src in enumerate((q, do)):
             remote(block(src, row, mine, grp), qd_l.at[w, 0, a, :, half(e), :], own_send.at[a], qd_recv.at[w, 0], dev)
         for a, src in enumerate((k, v)):
-            remote(src.at[row, mine], kv_l.at[w, c_own, a, half(e), :], own_send.at[2 + a], kv_recv.at[w, c_own], dev)
+            remote(src.at[row, half(mine)], kv_l.at[w, c_own, a, half(e), :], own_send.at[2 + a], kv_recv.at[w, c_own], dev)
 
     def feed_keys(w, lane, kind):
         for a, src in enumerate((k, v)):
-            remote(src.at[row_of(w, lane), 1 - head_of(kind)], kv_l.at[w, c_own, a, half(e), :],
+            remote(src.at[row_of(w, lane), half(1 - head_of(kind))], kv_l.at[w, c_own, a, half(e), :],
                    fed_send.at[2 + a], kv_recv.at[w, c_own], core(*feeder(kind), lane))
 
     def feed_queries(w, lane, kind):
@@ -245,7 +274,7 @@
         @pl.when(first_has_kv(kind))
         def _():
             for a, src in enumerate((k, v)):
-                remote(src.at[row_of(w, lane), head_of(kind)], kv_l.at[w, c_own, a, half(e), :],
+                remote(src.at[row_of(w, lane), half(head_of(kind))], kv_l.at[w, c_own, a, half(e), :],
                        kv_send.at[a], kv_recv.at[w, c_own], core(*partner(kind), lane))
 
     def fed_chunk(kind):
@@ -280,7 +309,7 @@
                 drain(other, kv_recv.at[w, j])
                 pltpu.make_async_copy(other, dst.at[:, half(1 - e), :], kv_load.at[w % 2, j]).start()
                 for a, src in enumerate((k, v)):
-                    pltpu.make_async_copy(src.at[row, mine], dst.at[a, half(e), :], kv_load.at[w % 2, j]).start()
+                    pltpu.make_async_copy(src.at[row, half(mine)], dst.at[a, half(e), :], kv_load.at[w % 2, j]).start()
 
             @pl.when(j != c_own)
             def _():
@@ -397,10 +426,13 @@
                 for lane in lanes:
                     job(w, lane, kind_of(w, lane))
 
+    for lane in range(2):
+        feed_queries(0, lane, kind_of(0, lane))
+    split_heads()
     first = [(4 * w - LEADS[j], w, j) for w in range(n_units) for j in range(len(jobs))]
     for h, w, j in sorted(first):
-        if h < 0:
-            job, lanes = jobs[j]
+        job, lanes = jobs[j]
+        if h < 0 and (w, job) != (0, feed_queries):
             for lane in lanes:
                 job(w, lane, kind_of(w, lane))
     fetch(0)
@@ -483,7 +515,7 @@
         @pl.when(first_has_kv(kind))
         def _():
             for a, src in enumerate((k, v)):
-                drain(src.at[0:sum(n_kind), 0], kv_send.at[a])
+                drain(src.at[0:sum(n_kind), 0:blk], kv_send.at[a])
 
         for lane in range(2):
             @pl.when(fed_goes_on(kind) & (e == lane))
@@ -557,14 +589,15 @@
         shape = jax.ShapeDtypeStruct
         q_shape = shape((n_rows, n_heads, blk, dim), bf16)
         k_shape = shape((n_rows, n_kv, blk, dim), bf16)
+        joined = shape((n_rows, blk * n_kv, dim), bf16)
         landing = (shape((n_units, 2, 2, grp, CHUNK, dim), bf16), shape((n_units, n_chunks, 2, CHUNK, dim), bf16),
                    shape((n_units, 2, 2, CHUNK, dim), f32))
         vmem, dma = pltpu.VMEM, pltpu.SemaphoreType.DMA
         res = pl.pallas_call(
             kernel,
-            out_shape=(q_shape, q_shape, k_shape, k_shape, *landing),
+            out_shape=(q_shape, q_shape, k_shape, k_shape, joined, joined, *landing),
             in_specs=[any_spec] * 4,
-            out_specs=(any_spec,) * 7,
+            out_specs=(any_spec,) * 9,
             scratch_shapes=[
                 vmem((2, 2, grp, CHUNK, dim), bf16), vmem((2, n_chunks, 2, CHUNK, dim), bf16),
                 vmem((OUT_SLOTS, 2, grp, CHUNK, dim), bf16),
@@ -583,8 +616,7 @@
             compiler_params=pltpu.CompilerParams(
                 collective_id=0, has_side_effects=True, vmem_limit_bytes=63 * 2**20),
             name='pair_attention',
-        )(*(to_heads(x) for x in (q_in, k_in, v_in, do_in)))
-        joined = shape((n_rows, blk * n_kv, dim), bf16)
+        )(to_heads(q_in), k_in.reshape(joined.shape), v_in.reshape(joined.shape), to_heads(do_in))
         o, dq, dk, dv = pl.pallas_call(
             finish_kernel,
             out_shape=(q_shape, q_shape, joined, joined),

time: 460 us -> 453 us (0.985)
  local copies, waits for them, and re-layouts: 7.18 us -> 0 us
    transpose x1 -> x0, local copies, waits for them, and re-layouts: 7.18 us -> none  [local_attn(): to_heads = lambda x: jnp.swapaxes(x, 1, 2)]
where the time goes in v5:
time: 453 us; the launch traced here: 452 us
  Pallas kernels  452 us (100%)
    pallas_call x1, Pallas kernels, local_attn(): pl.pallas_call(kernel, out_shape=(q_shape, q_shape, k_shape, k_shape, joi...  435 us
    pallas_call x1, Pallas kernels, local_attn(): pl.pallas_call(finish_kernel, out_shape=(q_shape, q_shape, joined, joined...  16.5 us

profile of v5, /device:TPU:5, one launch (start us, length us, event | category | flops | bytes accessed | tf_op | source)
XLA Modules:
  0.0 452.4 jit_solution(12221700407591823791)
XLA Ops:
  0.6 435.1 %pair_attention.1 = (bf16[16,6,384,128]{3,2,1,0:T(8,128)(2,1)}, bf16[16,6,384,128]{3,2,1,0:T(8,128)(2,1)}, bf16[16,2,384,128]{3,2,1,0:T(8,128)(2,1)}, bf16[16,2,...) custom-call(bf16[16,6,384,128]{3,2,1,0:T(8,128)(2,1)} %bitcast.8, ...), custom_call_target="tpu_custom_call" | custom-call | tf_op jit(solution)/shard_map/pair_attention/pallas_call | solution.py:596
  435.8 16.5 %finish.1 = (bf16[16,6,384,128]{3,2,1,0:T(8,128)(2,1)}, bf16[16,6,384,128]{3,2,1,0:T(8,128)(2,1)}, bf16[16,768,128]{2,1,0:T(8,128)(2,1)}, bf16[16,768,128]{2,1,0:T(8,128)(2,1)}) custom-call(bf16[16,6,384,128]{3,2,1,0:T(8,128)(2,1)} %get-tuple-element.12.o, bf16[16,6,384,128]{3,2,1,0:T(8,128)(2,1)} %get-tuple-element.13.dq, ...), custom_call_target="tpu_custom_call" | custom-call | tf_op jit(solution)/shard_map/finish/pallas_call | solution.py:620

commit v6 on v5

v6 whole, which is shorter than its diff:
```python
import functools
import math
import jax
import jax.numpy as jnp
from jax import lax
from jax.experimental import pallas as pl
from jax.experimental.pallas import tpu as pltpu
from jax.sharding import PartitionSpec as P

CTX_AXES = ('ctxo', 'ctx')
MESH = pl.DeviceIdType.MESH
f32 = jnp.float32
bf16 = jnp.bfloat16
CHUNK = 768
SUB = 256
def by_chip(rows, read):
    return {kind: {c: read(word) for c, word in enumerate(words.split()) if word != '-'} for kind, words in rows.items()}


def digits(word):
    return tuple(int(z) for z in word)


WORK = by_chip({'T': '02 13 - -', 'Y': '0 - 2 13', 'X': '01 - 23 -', 'V': '0 1 - 23'}, digits)
FEED = by_chip({'T': '- - 0 1', 'Y': '- 3 - -', 'X': '- 0 - 2', 'V': '- - 3 -'}, int)
SHARE = by_chip({'T': '1 0 - -', 'Y': '2 - 3 -', 'X': '2 - - -', 'V': '1 3 - -'}, digits)
RELAY = by_chip({'T': '21 - - -', 'Y': '- - 03 12', 'X': '12 - - -', 'V': '- 03 - -'}, digits)
SUMS = by_chip({'T': '110 201000 - -', 'Y': '022 - 130 221020', 'X': '- - 000101 -', 'V': '012 - - 010111'},
               lambda word: tuple(digits(word[i:i + 3]) for i in range(0, len(word), 3)))
FINISH = by_chip({'T': '02:0:1 13:0: - -', 'Y': '- - 02:02:1 13:0:', 'X': '01:0:1 - 23:: -', 'V': '- 01:02:1 - 23::'},
                 lambda word: tuple(digits(part) for part in word.split(':')))
KINDS = 'TYXV'
UNITS = ('VTYXYTTVXXTVTVYX', 'VXYTTYXVXYTTVXTV')
LEADS = (20, 27, 20, 10, 10)
LAG = 2
OUT_SLOTS = 4


def dot(a, b):
    return jnp.dot(a, b, preferred_element_type=f32)


def fold(x, op):
    return op(x.reshape(x.shape[0] // 8, 8, x.shape[1]), axis=0)


def tile(i):
    return slice(i * SUB, (i + 1) * SUB)


def attend_chunk(c, q, do, kv, o, dq, g, base, s, scale, hooks):
    kT, vT, qT, doT, sc_ref, dp_ref, oT, dqT, pb, sb = s
    score_scale = scale * math.log2(math.e)
    n_sub = CHUNK // SUB
    n_heads = q.shape[0]

    def cols(ki, diag):
        return range(ki, n_sub) if diag else range(n_sub)

    lowest = tuple(jnp.full((8, SUB), -jnp.inf, f32) for _ in range(n_sub))

    def load_heads(h, b):
        for i in range(n_sub):
            qT[b, :, tile(i)] = q[h, tile(i), :].T
            doT[b, :, tile(i)] = do[h, tile(i), :].T

    def scores(j, b, m, ki, diag):
        for qi in cols(ki, diag):
            x = dot(kv[j, 0, tile(ki), :], qT[b, :, tile(qi)]) * score_scale
            if diag and ki == qi:
                key = lax.broadcasted_iota(jnp.int32, (SUB, SUB), 0)
                query = lax.broadcasted_iota(jnp.int32, (SUB, SUB), 1)
                x = jnp.where(key <= query, x, -jnp.inf)
            sc_ref[b, j, tile(ki), tile(qi)] = x
            m[qi] = jnp.maximum(m[qi], fold(x, jnp.max))

    def score_pass(b):
        def body(j, m, diag=False):
            m = list(m)
            for ki in range(n_sub):
                scores(j, b, m, ki, diag)
            return tuple(m)
        return body(c, lax.fori_loop(0, c, body, lowest), True)

    def forward_pass(b, m):
        top = [jnp.max(x, axis=0, keepdims=True) for x in m]
        oT[...] = jnp.zeros_like(oT)

        def body(j, l, diag=False):
            l, acc = list(l), [None] * n_sub

            def probs(ki):
                for qi in cols(ki, diag):
                    e = jnp.exp2(sc_ref[b, j, tile(ki), tile(qi)] - top[qi])
                    sc_ref[b, j, tile(ki), tile(qi)] = e
                    l[qi] = l[qi] + fold(e, jnp.sum)
                    pb[ki % 2, :, tile(qi)] = e.astype(bf16)

            def prob_grads(ki):
                for qi in cols(ki, diag):
                    dp_ref[j, tile(ki), tile(qi)] = dot(kv[j, 1, tile(ki), :], doT[b, :, tile(qi)])

            def outputs(ki):
                for qi in cols(ki, diag):
                    d = dot(vT[j, :, tile(ki)], pb[ki % 2, :, tile(qi)])
                    acc[qi] = d if acc[qi] is None else acc[qi] + d

            for ki in range(n_sub + 1):
                if ki < n_sub:
                    prob_grads(ki)
                    probs(ki)
                if ki:
                    outputs(ki - 1)
            for qi in range(n_sub):
                oT[:, tile(qi)] += acc[qi]
            return tuple(l)

        l = tuple(jnp.zeros((8, SUB), f32) for _ in range(n_sub))
        l = body(c, lax.fori_loop(0, c, body, l), True)
        return [1.0 / jnp.sum(x, axis=0, keepdims=True) for x in l]

    def finish_outputs(h, b, inv):
        drow = []
        for qi in range(n_sub):
            out = oT[:, tile(qi)] * inv[qi]
            drow.append(jnp.sum(out * doT[b, :, tile(qi)].astype(f32), axis=0, keepdims=True))
            o[h, tile(qi), :] = out.astype(bf16).T
        return drow

    def backward_pass(h, b, inv, drow, more):
        dqT[...] = jnp.zeros_like(dqT)

        def body(j, m, diag=False):
            m, acc = list(m), [None] * n_sub

            def score_grads(ki):
                for qi in cols(ki, diag):
                    p = sc_ref[b, j, tile(ki), tile(qi)] * inv[qi]
                    ds = p * (dp_ref[j, tile(ki), tile(qi)] - drow[qi])
                    pb[ki % 2, :, tile(qi)] = p.astype(bf16)
                    sb[ki % 2, :, tile(qi)] = ds.astype(bf16)

            def grads(ki):
                first = ki * SUB if diag else 0
                for qi in cols(ki, diag):
                    d = dot(kT[j, :, tile(ki)], sb[ki % 2, :, tile(qi)])
                    acc[qi] = d if acc[qi] is None else acc[qi] + d
                g[base + j, 1, tile(ki), :] += dot(pb[ki % 2, :, first:], do[h, first:, :])
                g[base + j, 0, tile(ki), :] += dot(sb[ki % 2, :, first:], q[h, first:, :])

            if more:
                scores(j, 1 - b, m, 0, diag)
            score_grads(0)
            for ki in range(1, n_sub):
                score_grads(ki)
                grads(ki - 1)
                if more:
                    scores(j, 1 - b, m, ki, diag)
            grads(n_sub - 1)
            for qi in range(n_sub):
                dqT[:, tile(qi)] += acc[qi]
            return tuple(m)

        m = body(c, lax.fori_loop(0, c, body, lowest), True)
        for qi in range(n_sub):
            dq[h, tile(qi), :] = (dqT[:, tile(qi)] * scale).astype(bf16).T
        return m

    load_heads(0, 0)
    m = score_pass(0)
    for h in range(n_heads):
        b = h % 2
        inv = forward_pass(b, m)
        drow = finish_outputs(h, b, inv)
        if h + 1 < n_heads:
            load_heads(h + 1, 1 - b)
        m = backward_pass(h, b, inv, drow, h + 1 < n_heads)
        if h < len(hooks):
            hooks[h]()


def kernel(q, k_raw, v_raw, do, o, dq, dk, dv, k, v, qd_l, kv_l, g_l,
           qd_v, kv_v, od_v, acc, g_in, g_out, kT, vT, *rest):
    scratch, sems = rest[:8], rest[8:]
    own_send, fed_send, kv_send, relay_send, qd_recv, kv_recv, g_send, g_recv, out_send, out_recv, grad_send, qd_load, kv_load, g_load = sems
    y, b = lax.axis_index('ctxo'), lax.axis_index('ctx')
    x, e = b // 2, b % 2
    chip = 2 * y + x
    n_rows, n_heads, blk, dim = q.shape
    n_kv = k.shape[1] // blk
    grp = n_heads // n_kv
    lane_rows = n_rows // 2
    n_units = lane_rows * n_kv
    chips, lanes = range(4), range(2)
    scale = 1.0 / math.sqrt(dim)
    depth = LAG + 1

    def core(c, ce):
        return (0, c // 2, 2 * (c % 2) + ce)

    def row_of(n, lane):
        return lane * lane_rows + n // n_kv

    def half(h):
        return pl.ds(pl.multiple_of(h * blk, blk), blk)

    def remote(src, dst, send, recv, dev):
        pltpu.make_async_remote_copy(src, dst, send, recv, device_id=dev, device_id_type=MESH).start()

    def drain(ref, sem):
        pltpu.make_async_copy(ref, ref, sem).wait()

    def choose(values, index):
        return functools.reduce(lambda r, i: jnp.where(index == i, values[i], r), range(1, len(values)), values[0])

    def tasks_of(c, lane):
        return [(n, j) for n in range(n_units) for j in WORK[UNITS[lane][n]].get(c, ())]

    def finished_of(c, lane):
        return [n for n in range(n_units) if c in FINISH[UNITS[lane][n]]]

    def here(value):
        return choose([value(c, lane) for c in chips for lane in lanes], 2 * chip + e)

    def padded(items, i):
        return items[i] if i < len(items) else 0
    most = max(len(tasks_of(c, lane)) for c in chips for lane in lanes)
    n_tasks = here(lambda c, lane: len(tasks_of(c, lane)))
    task_tab = [here(lambda c, lane: padded([4 * n + j for n, j in tasks_of(c, lane)], i)) for i in range(most + 1)]
    start_tab = [here(lambda c, lane: sum(m < n for m, _ in tasks_of(c, lane))) for n in range(n_units)]
    n_finished = here(lambda c, lane: len(finished_of(c, lane)))
    fin_tab = [here(lambda c, lane: padded(finished_of(c, lane), i)) for i in range(n_units)]

    def units_before(c, lane, i, finished):
        tasks = tasks_of(c, lane)
        now = tasks[i][0] if i < len(tasks) else n_units
        return sum((n in finished_of(c, lane)) == finished for n in {m for m, _ in tasks if m < now})
    fin_before = [here(lambda c, lane: units_before(c, lane, i, True)) for i in range(most)]
    oth_before = [here(lambda c, lane: units_before(c, lane, i, False)) for i in range(most)]

    def kind_of(n, lane):
        return jnp.where(lane == 0, *(choose([KINDS.index(u) for u in UNITS[c]], n) for c in lanes))

    def role(table, kind, c=chip):
        return choose([table(u, i) for u in KINDS for i in chips], 4 * kind + c)

    def own(kind):
        return role(lambda u, c: int(c in WORK[u].get(c, ())), kind) == 1

    def relayed(kind):
        return role(lambda u, c: RELAY[u].get(c, (-1, 0))[0], kind)

    barrier = pltpu.get_barrier_semaphore()
    peers = [core(chip, 1 - e)] + [core(c, ce) for c in (2 * (1 - y) + x, 2 * y + 1 - x) for ce in lanes]
    for dev in peers:
        pl.semaphore_signal(barrier, inc=1, device_id=dev, device_id_type=MESH)
    pl.semaphore_wait(barrier, len(peers))

    def block(src, n, lane, a):
        if a < 2:
            return src.at[row_of(n, lane), pl.ds((n % n_kv) * grp, grp)]
        return src.at[row_of(n, lane), half(n % n_kv)]

    def split_heads():
        part = SUB // n_kv
        at = lax.broadcasted_iota(jnp.int32, (SUB, SUB), 0)
        take = lax.broadcasted_iota(jnp.int32, (SUB, SUB), 1)
        perm = jnp.where(take == (at % part) * n_kv + at // part, 1.0, 0.0).astype(bf16)

        def room(a, r):
            return od_v.at[r // 6, r // 3 % 2, r % 3] if a else kv_v.at[r // 8, r // 2 % 4, r % 2]

        for a, raw in enumerate((k_raw, v_raw)):
            for r in range(n_rows):
                pltpu.make_async_copy(raw.at[r], room(a, r), kv_load.at[a, r // 4]).start()
        for a, (raw, dst) in enumerate(((k_raw, k), (v_raw, v))):
            def sort(r, _):
                @pl.when(r % 4 == 0)
                def _():
                    drain(raw.at[0:4], kv_load.at[a, r // 4])
                x = room(a, r)
                y = [dot(perm, x[tile(p), :]).astype(bf16) for p in range(n_kv * blk // SUB)]
                for p, rows in enumerate(y):
                    for h in range(n_kv):
                        x[h * blk + p * part:h * blk + (p + 1) * part, :] = rows[h * part:(h + 1) * part]
                return 0
            lax.fori_loop(0, n_rows, sort, 0)
            for r in range(n_rows):
                pltpu.make_async_copy(room(a, r), dst.at[r], qd_load.at[a]).start()
        for a, dst in enumerate((k, v)):
            drain(dst, qd_load.at[a])

    def send_keys(n, lane, c, send):
        for a, src in enumerate((k, v)):
            remote(block(src, n, lane, 2), kv_l.at[n, chip, a, half(e), :], send(a), kv_recv.at[n, chip], core(c, lane))

    def send_queries(n, lane, c, place, send):
        for a, src in enumerate((q, do)):
            remote(block(src, n, lane, 0), qd_l.at[n, place, a, :, half(e), :], send(a), qd_recv.at[n, place], core(c, lane))

    def send_own(n):
        lane = 1 - e

        @pl.when(own(kind_of(n, lane)))
        def _():
            send_queries(n, lane, chip, 0, lambda a: own_send.at[a])
            send_keys(n, lane, chip, lambda a: own_send.at[2 + a])

    def feed_keys(n):
        for lane in lanes:
            c = role(lambda u, i: FEED[u].get(i, -1), kind_of(n, lane))

            @pl.when(c >= 0)
            def _():
                send_keys(n, lane, c, lambda a: fed_send.at[2 + a, lane])

    def feed_queries(n):
        for lane in lanes:
            c = role(lambda u, i: FEED[u].get(i, -1), kind_of(n, lane))

            @pl.when(c >= 0)
            def _():
                send_queries(n, lane, c, 1, lambda a: fed_send.at[a, lane])

    def share_keys(n):
        for lane in lanes:
            c = role(lambda u, i: SHARE[u].get(i, (-1,))[0], kind_of(n, lane))

            @pl.when(c >= 0)
            def _():
                send_keys(n, lane, c, lambda a: kv_send.at[a, lane])

    def pass_on(n):
        kind = kind_of(n, e)
        j = relayed(kind)

        @pl.when(j >= 0)
        def _():
            drain(kv_l.at[n, j], kv_recv.at[n, j])
            c = role(lambda u, i: RELAY[u].get(i, (0, 0))[1], kind)
            remote(kv_l.at[n, j], kv_l.at[n, j], relay_send, kv_recv.at[n, j], core(c, e))

    jobs = (send_own, share_keys, feed_keys, pass_on, feed_queries)
    early_units = n_kv

    def run_due(h):
        for job, lead in zip(jobs, LEADS):
            lo = sum(jnp.where(2 * t - lead < h, 1, 0) for t in start_tab)
            hi = sum(jnp.where(2 * t - lead < h + 1, 1, 0) for t in start_tab)
            if job is feed_queries:
                lo = jnp.where(lo < early_units, early_units, lo)

            def one(n, _):
                job(n)
                return 0
            lax.fori_loop(lo, hi, one, 0)

    def fetch(s, slot_kv, first, prev):
        code = choose(task_tab, s)
        n, c = code // 4, code % 4
        kind, slot = kind_of(n, e), s % 2

        def keys(j, _):
            dst, sem = kv_v.at[slot_kv, j], kv_load.at[slot_kv, j]

            @pl.when(j == chip)
            def _():
                other = kv_l.at[n, j, :, half(1 - e), :]
                drain(other, kv_recv.at[n, j])
                pltpu.make_async_copy(other, dst.at[:, half(1 - e), :], sem).start()
                for a, src in enumerate((k, v)):
                    pltpu.make_async_copy(block(src, n, e, 2), dst.at[a, half(e), :], sem).start()

            @pl.when(j != chip)
            def _():
                @pl.when(j != relayed(kind))
                def _():
                    drain(kv_l.at[n, j], kv_recv.at[n, j])
                pltpu.make_async_copy(kv_l.at[n, j], dst, sem).start()
            return 0
        lax.fori_loop(jnp.where(first, 0, prev + 1), c + 1, keys, 0)

        @pl.when(c == chip)
        def _():
            other = qd_l.at[n, 0, :, :, half(1 - e), :]
            drain(other, qd_recv.at[n, 0])
            pltpu.make_async_copy(other, qd_v.at[slot, :, :, half(1 - e), :], qd_load.at[slot]).start()
            for a, src in enumerate((q, do)):
                pltpu.make_async_copy(block(src, n, e, 0), qd_v.at[slot, a, :, half(e), :], qd_load.at[slot]).start()

        @pl.when(c != chip)
        def _():
            drain(qd_l.at[n, 1], qd_recv.at[n, 1])
            pltpu.make_async_copy(qd_l.at[n, 1], qd_v.at[slot], qd_load.at[slot]).start()

    def place(c, send, pieces):
        for h in range(2):
            local = (c == chip) & (e == h)
            for src, dst, recv in pieces(h):
                @pl.when(local)
                def _():
                    pltpu.make_async_copy(src, dst, send).start()

                @pl.when(jnp.logical_not(local))
                def _():
                    remote(src, dst, send, recv, core(c, h))

    def n_in(kind, f):
        return role(lambda u, c: len(FINISH[u][c][1 + f]) if c in FINISH[u] else 0, kind)

    def get_sums(n, a):
        drain(g_l.at[n, a], g_recv.at[n, a])
        pltpu.make_async_copy(g_l.at[n, a], g_in.at[a], g_load.at[a]).start()

    def fetch_sums(i):
        n = choose(fin_tab, i)
        kind = kind_of(n, e)
        for a, f, least in ((0, 0, 1), (2, 0, 2), (1, 1, 1)):
            @pl.when(n_in(kind, f) >= least)
            def _():
                get_sums(n, a)

    def merge(i):
        n = choose(fin_tab, i)
        kind, base, slot = kind_of(n, e), 4 * (i % depth), i % 2
        for f in range(2):
            c = role(lambda u, j: FINISH[u][j][0][f] if j in FINISH[u] else 0, kind)

            @pl.when(i >= 2)
            def _():
                drain(g_out.at[slot, f], grad_send.at[slot, f])
            for places in ((), (0,), (0, 2)) if f == 0 else ((), (1,)):
                @pl.when(n_in(kind, f) == len(places))
                def _():
                    for a in places:
                        drain(g_in.at[a], g_load.at[a])
                    for i_kv, factor in enumerate((scale, None)):
                        total = acc[base + c, i_kv]
                        for a in places:
                            total = total + g_in[a, i_kv]
                        g_out[slot, f, i_kv] = (total if factor is None else total * factor).astype(bf16)
            place(c, grad_send.at[slot, f], lambda h: [
                (g_out.at[slot, f, i_kv, h * blk:(h + 1) * blk, :], dst.at[row_of(n, e), n % n_kv], out_recv.at[2 + i_kv, e])
                for i_kv, dst in enumerate((dk, dv))])

    def n_sums(kind):
        return role(lambda u, c: len(SUMS[u].get(c, ())), kind)

    def send_sums(n, base, sem):
        kind = kind_of(n, e)
        for m in range(2):
            @pl.when(n_sums(kind) > m)
            def _():
                j, c, a = (role(lambda u, i: SUMS[u][i][m][part] if len(SUMS[u].get(i, ())) > m else 0, kind) for part in range(3))
                remote(acc.at[base + j], g_l.at[n, a], sem, g_recv.at[n, a], core(c, e))

    def sums_left(i):
        n = choose(fin_tab, i)
        for m in (1, 2):
            @pl.when(n_sums(kind_of(n, e)) == m)
            def _():
                drain(acc.at[0:m], g_send.at[i % depth])

    lax.fori_loop(0, early_units, lambda n, _: (feed_queries(n), 0)[1], 0)
    split_heads()

    def before(h, _):
        run_due(h - max(LEADS))
        return 0
    lax.fori_loop(0, max(LEADS), before, 0)
    fetch(0, 0, True, 0)

    def task(s, _):
        n_fin, n_oth = choose(fin_before, s), choose(oth_before, s)
        code, after = choose(task_tab, s), choose(task_tab, s + 1)
        n, c = code // 4, code % 4
        prev = choose([task_tab[0]] + task_tab[:-1], s)
        first = (s == 0) | (prev // 4 != n)
        last = (s + 1 == n_tasks) | (after // 4 != n)
        kind = kind_of(n, e)
        fin = role(lambda u, i: int(i in FINISH[u]), kind) == 1
        base = jnp.where(fin, 4 * (n_fin % depth), 4 * depth + n_oth % 2)
        slot, slot_kv, o_slot = s % 2, (n_fin + n_oth) % 2, s % OUT_SLOTS
        lo = jnp.where(first, 0, prev % 4 + 1)

        @pl.when(first & fin & (n_fin >= depth))
        def _():
            sums_left(n_fin - depth)

        @pl.when(first & jnp.logical_not(fin) & (n_oth >= 2))
        def _():
            drain(acc.at[0], g_send.at[depth + n_oth % 2])

        def turn(j, _):
            drain(kv_v.at[slot_kv, j], kv_load.at[slot_kv, j])
            kT[j] = kv_v[slot_kv, j, 0].T
            vT[j] = kv_v[slot_kv, j, 1].T
            acc[base + j] = jnp.zeros(acc.shape[1:], f32)
            return 0
        lax.fori_loop(lo, c + 1, turn, 0)
        drain(qd_v.at[slot], qd_load.at[slot])

        @pl.when(s >= OUT_SLOTS)
        def _():
            drain(od_v.at[o_slot], out_send.at[o_slot])

        def early():
            run_due(2 * s)

        def late():
            run_due(2 * s + 1)

            @pl.when(s + 1 < n_tasks)
            def _():
                fetch(s + 1, (n_fin + n_oth + jnp.where(last, 1, 0)) % 2, last, c)

            @pl.when(last & fin & (n_fin >= LAG))
            def _():
                fetch_sums(n_fin - LAG)
        attend_chunk(c, qd_v.at[slot, 0], qd_v.at[slot, 1], kv_v.at[slot_kv], od_v.at[o_slot, 0], od_v.at[o_slot, 1],
                     acc, base, (kT, vT, *scratch), scale, (early, late))
        place(c, out_send.at[o_slot], lambda h: [
            (od_v.at[o_slot, i, :, h * blk:(h + 1) * blk, :], block(dst, n, e, 0), out_recv.at[i, e]) for i, dst in enumerate((o, dq))])

        @pl.when(last)
        def _():
            send_sums(n, base, g_send.at[jnp.where(fin, n_fin % depth, depth + n_oth % 2)])

            @pl.when(fin & (n_fin >= LAG))
            def _():
                merge(n_fin - LAG)
        return 0

    def task_or_rest(s, _):
        @pl.when(s < n_tasks)
        def _():
            task(s, 0)
        return 0
    lax.fori_loop(0, most, task_or_rest, 0)

    def rest_of(i, _):
        fetch_sums(i)
        merge(i)
        return 0
    lax.fori_loop(n_finished - LAG, n_finished, rest_of, 0)

    for slot in range(OUT_SLOTS):
        drain(od_v.at[slot], out_send.at[slot])
    for slot in range(2):
        for f in range(2):
            drain(g_out.at[slot, f], grad_send.at[slot, f])
    lax.fori_loop(n_finished - depth, n_finished, lambda i, _: (sums_left(i), 0)[1], 0)

    def count(table, c, lane):
        return sum(int(table(UNITS[lane][n], c)) for n in range(n_units))

    def wait_blocks(m, sem, ref):
        if m:
            drain(ref(m), sem)

    for d in range(8):
        c, lane = d // 2, d % 2

        @pl.when(2 * chip + e == d)
        def _():
            queries = [lambda m, src=src: src.at[0:m, pl.ds(0, grp)] for src in (q, do, o, dq)]
            keys = [lambda m, src=src: src.at[0:m, pl.ds(0, blk)] for src in (k, v)]
            grads = [lambda m, src=src: src.at[0:m, 0] for src in (dk, dv)]
            for a, ref in enumerate(queries[:2] + keys):
                wait_blocks(count(lambda u, i: i in WORK[u].get(i, ()), c, 1 - lane), own_send.at[a], ref)
                for ln in lanes:
                    wait_blocks(count(lambda u, i: i in FEED[u], c, ln), fed_send.at[a, ln], ref)
            for a, ref in enumerate(keys):
                for ln in lanes:
                    wait_blocks(count(lambda u, i: i in SHARE[u], c, ln), kv_send.at[a, ln], ref)
            wait_blocks(count(lambda u, i: i in RELAY[u], c, lane), relay_send, lambda m: kv_l.at[0:m, 0])
            for a, ref in enumerate(queries[2:] + grads):
                for ln in lanes:
                    at_home = (lambda u, i: i in WORK[u].get(i, ())) if a < 2 else (lambda u, i: i in FINISH[u] and i in FINISH[u][i][0])
                    wait_blocks(n_units - (count(at_home, c, ln) if ln == lane else 0), out_recv.at[a, ln], ref)
    for d in range(8):
        left = [n for n in range(n_units) if d // 2 in WORK[UNITS[d % 2][n]] and d // 2 not in FINISH[UNITS[d % 2][n]]]
        for i in range(max(len(left) - 2, 0), len(left)):
            @pl.when(2 * chip + e == d)
            def _():
                drain(acc.at[0], g_send.at[depth + i % 2])


def finish_kernel(o, dq, dk, dv, o_out, dq_out, dk_out, dv_out, ring, g_in, g_out, ring_in, ring_out, g_load, g_store):
    n_rows, n_kv, blk, _ = dk.shape
    half = SUB // n_kv
    at = lax.broadcasted_iota(jnp.int32, (SUB, SUB), 0)
    take = lax.broadcasted_iota(jnp.int32, (SUB, SUB), 1)
    perm = jnp.where(take == (at % n_kv) * half + at // n_kv, 1.0, 0.0).astype(bf16)
    pairs = ((o, o_out), (dq, dq_out))
    grads = ((dk, dk_out), (dv, dv_out))

    def move(i, out):
        src, dst = pairs[i % 2]
        if out:
            return pltpu.make_async_copy(ring.at[i], dst.at[i // 2], ring_out.at[i])
        return pltpu.make_async_copy(src.at[i // 2], ring.at[i], ring_in.at[i])

    def grad_rows(r):
        return pl.ds(4 * (r // 4), 4)

    def load(a, r):
        return pltpu.make_async_copy(grads[a][0].at[grad_rows(r)], g_in.at[a, grad_rows(r)], g_load.at[a, r // 4])

    def store(a, r):
        return pltpu.make_async_copy(g_out.at[a, grad_rows(r)], grads[a][1].at[grad_rows(r)], g_store.at[a, r // 4])

    n = 2 * n_rows
    for i in range(4):
        move(i, False).start()
    for r in range(0, n_rows, 4):
        load(0, r).start()
        load(1, r).start()
    for i in range(4, n):
        move(i, False).start()
    for i in range(n):
        move(i, False).wait()
        move(i, True).start()
        a, r = i % 2, i // 2
        if r % 4 == 0:
            load(a, r).wait()
        for p in range(blk // half):
            x = jnp.concatenate([g_in[a, r, h, p * half:(p + 1) * half, :] for h in range(n_kv)], 0)
            g_out[a, r, p * SUB:(p + 1) * SUB, :] = dot(perm, x).astype(bf16)
        if r % 4 == 3:
            store(a, r).start()
    for i in range(n):
        move(i, True).wait()
    for r in range(0, n_rows, 4):
        store(0, r).wait()
        store(1, r).wait()


def solution(mesh):
    spec = P('data', CTX_AXES, None, None)

    def local_attn(q_in, k_in, v_in, do_in):
        n_rows, blk, n_heads, dim = q_in.shape
        n_kv = k_in.shape[2]
        grp = n_heads // n_kv
        n_units = n_rows // 2 * n_kv
        n_chunks = 4
        to_heads = lambda x: jnp.swapaxes(x, 1, 2)
        any_spec = pl.BlockSpec(memory_space=pl.ANY)
        shape = jax.ShapeDtypeStruct
        q_shape = shape((n_rows, n_heads, blk, dim), bf16)
        k_shape = shape((n_rows, n_kv, blk, dim), bf16)
        joined = shape((n_rows, blk * n_kv, dim), bf16)
        landing = (shape((n_units, 2, 2, grp, CHUNK, dim), bf16), shape((n_units, n_chunks, 2, CHUNK, dim), bf16),
                   shape((n_units, 3, 2, CHUNK, dim), f32))
        vmem, dma = pltpu.VMEM, pltpu.SemaphoreType.DMA
        res = pl.pallas_call(
            kernel,
            out_shape=(q_shape, q_shape, k_shape, k_shape, joined, joined, *landing),
            in_specs=[any_spec] * 4,
            out_specs=(any_spec,) * 9,
            scratch_shapes=[
                vmem((2, 2, grp, CHUNK, dim), bf16), vmem((2, n_chunks, 2, CHUNK, dim), bf16),
                vmem((OUT_SLOTS, 2, grp, CHUNK, dim), bf16),
                vmem(((LAG + 1) * n_chunks + 2, 2, CHUNK, dim), f32),
                vmem((3, 2, CHUNK, dim), f32), vmem((2, 2, 2, CHUNK, dim), bf16),
                vmem((n_chunks, dim, CHUNK), bf16), vmem((n_chunks, dim, CHUNK), bf16),
                vmem((2, dim, CHUNK), bf16), vmem((2, dim, CHUNK), bf16),
                vmem((2, n_chunks, CHUNK, CHUNK), f32), vmem((n_chunks, CHUNK, CHUNK), f32),
                vmem((dim, CHUNK), f32), vmem((dim, CHUNK), f32),
                vmem((2, SUB, CHUNK), bf16), vmem((2, SUB, CHUNK), bf16),
                dma((4,)), dma((4, 2)), dma((2, 2)), dma,
                dma((n_units, 2)), dma((n_units, n_chunks)),
                dma((LAG + 3,)), dma((n_units, 3)),
                dma((OUT_SLOTS,)), dma((4, 2)), dma((2, 2)), dma((2,)), dma((2, n_chunks)), dma((3,)),
            ],
            compiler_params=pltpu.CompilerParams(
                collective_id=0, has_side_effects=True, vmem_limit_bytes=63 * 2**20),
            name='pair_attention',
        )(to_heads(q_in), k_in.reshape(joined.shape), v_in.reshape(joined.shape), to_heads(do_in))
        o, dq, dk, dv = pl.pallas_call(
            finish_kernel,
            out_shape=(q_shape, q_shape, joined, joined),
            in_specs=[any_spec] * 4,
            out_specs=(any_spec,) * 4,
            scratch_shapes=[
                vmem((2 * n_rows, n_heads, blk, dim), bf16),
                vmem((2, n_rows, n_kv, blk, dim), bf16), vmem((2, n_rows, n_kv * blk, dim), bf16),
                dma((2 * n_rows,)), dma((2 * n_rows,)), dma((2, n_rows // 4)), dma((2, n_rows // 4)),
            ],
            compiler_params=pltpu.CompilerParams(vmem_limit_bytes=62 * 2**20),
            name='finish',
        )(*res[:4])
        return to_heads(o), to_heads(dq), dk.reshape(k_in.shape), dv.reshape(k_in.shape)

    return jax.shard_map(local_attn, mesh=mesh, in_specs=(spec,) * 4, out_specs=(spec,) * 4, check_vma=False)
```

time: 453 us -> 439 us (0.969)
  Pallas kernels: 452 us -> 435 us
    pallas_call x1, Pallas kernels: 435 us -> 418 us  [local_attn(): pl.pallas_call(kernel, out_shape=(q_shape, q_shape, k_shape, k_shape, joi...]
where the time goes in v6:
time: 439 us; the launch traced here: 435 us
  Pallas kernels  435 us (99%)
    pallas_call x1, Pallas kernels, local_attn(): pl.pallas_call(kernel, out_shape=(q_shape, q_shape, k_shape, k_shape, joi...  418 us
    pallas_call x1, Pallas kernels, local_attn(): pl.pallas_call(finish_kernel, out_shape=(q_shape, q_shape, joined, joined...  16.4 us

profile of v6, /device:TPU:5, one launch (start us, length us, event | category | flops | bytes accessed | tf_op | source)
XLA Modules:
  0.0 435.4 jit_solution(12442174079336930464)
XLA Ops:
  0.6 418.1 %pair_attention.1 = (bf16[16,6,384,128]{3,2,1,0:T(8,128)(2,1)}, bf16[16,6,384,128]{3,2,1,0:T(8,128)(2,1)}, bf16[16,2,384,128]{3,2,1,0:T(8,128)(2,1)}, bf16[16,2,...) custom-call(bf16[16,6,384,128]{3,2,1,0:T(8,128)(2,1)} %bitcast.8, ...), custom_call_target="tpu_custom_call" | custom-call | tf_op jit(solution)/shard_map/pair_attention/pallas_call | solution.py:657
  418.8 16.4 %finish.1 = (bf16[16,6,384,128]{3,2,1,0:T(8,128)(2,1)}, bf16[16,6,384,128]{3,2,1,0:T(8,128)(2,1)}, bf16[16,768,128]{2,1,0:T(8,128)(2,1)}, bf16[16,768,128]{2,1,0:T(8,128)(2,1)}) custom-call(bf16[16,6,384,128]{3,2,1,0:T(8,128)(2,1)} %get-tuple-element.12.o, bf16[16,6,384,128]{3,2,1,0:T(8,128)(2,1)} %get-tuple-element.13.dq, ...), custom_call_target="tpu_custom_call" | custom-call | tf_op jit(solution)/shard_map/finish/pallas_call | solution.py:681

commit v7 on v6

--- a/solution.py
+++ b/solution.py
@@ -30,8 +30,8 @@
 FINISH = by_chip({'T': '02:0:1 13:0: - -', 'Y': '- - 02:02:1 13:0:', 'X': '01:0:1 - 23:: -', 'V': '- 01:02:1 - 23::'},
                  lambda word: tuple(digits(part) for part in word.split(':')))
 KINDS = 'TYXV'
-UNITS = ('VTYXYTTVXXTVTVYX', 'VXYTTYXVXYTTVXTV')
-LEADS = (20, 27, 20, 10, 10)
+UNITS = ('TVXYTVXTYXTYXYVT', 'XTVXTVYXTYTYXVTX')
+LEADS = (20, 25, 21, 10, 7)
 LAG = 2
 OUT_SLOTS = 4
 

time: 439 us -> 431 us (0.982)
  Pallas kernels: 435 us -> 425 us
    pallas_call x1, Pallas kernels: 418 us -> 408 us  [local_attn(): pl.pallas_call(kernel, out_shape=(q_shape, q_shape, k_shape, k_shape, joi...]
where the time goes in v7:
time: 431 us; the launch traced here: 425 us
  Pallas kernels  425 us (99%)
    pallas_call x1, Pallas kernels, local_attn(): pl.pallas_call(kernel, out_shape=(q_shape, q_shape, k_shape, k_shape, joi...  408 us
    pallas_call x1, Pallas kernels, local_attn(): pl.pallas_call(finish_kernel, out_shape=(q_shape, q_shape, joined, joined...  16.4 us

profile of v7, /device:TPU:5, one launch (start us, length us, event | category | flops | bytes accessed | tf_op | source)
XLA Modules:
  0.0 425.4 jit_solution(4087266453534827952)
XLA Ops:
  0.6 408.1 %pair_attention.1 = (bf16[16,6,384,128]{3,2,1,0:T(8,128)(2,1)}, bf16[16,6,384,128]{3,2,1,0:T(8,128)(2,1)}, bf16[16,2,384,128]{3,2,1,0:T(8,128)(2,1)}, bf16[16,2,...) custom-call(bf16[16,6,384,128]{3,2,1,0:T(8,128)(2,1)} %bitcast.8, ...), custom_call_target="tpu_custom_call" | custom-call | tf_op jit(solution)/shard_map/pair_attention/pallas_call | solution.py:657
  408.8 16.4 %finish.1 = (bf16[16,6,384,128]{3,2,1,0:T(8,128)(2,1)}, bf16[16,6,384,128]{3,2,1,0:T(8,128)(2,1)}, bf16[16,768,128]{2,1,0:T(8,128)(2,1)}, bf16[16,768,128]{2,1,0:T(8,128)(2,1)}) custom-call(bf16[16,6,384,128]{3,2,1,0:T(8,128)(2,1)} %get-tuple-element.12.o, bf16[16,6,384,128]{3,2,1,0:T(8,128)(2,1)} %get-tuple-element.13.dq, ...), custom_call_target="tpu_custom_call" | custom-call | tf_op jit(solution)/shard_map/finish/pallas_call | solution.py:681

commit v8 on v7

--- a/solution.py
+++ b/solution.py
@@ -513,10 +513,6 @@
             @pl.when(s + 1 < n_tasks)
             def _():
                 fetch(s + 1, (n_fin + n_oth + jnp.where(last, 1, 0)) % 2, last, c)
-
-            @pl.when(last & fin & (n_fin >= LAG))
-            def _():
-                fetch_sums(n_fin - LAG)
         attend_chunk(c, qd_v.at[slot, 0], qd_v.at[slot, 1], kv_v.at[slot_kv], od_v.at[o_slot, 0], od_v.at[o_slot, 1],
                      acc, base, (kT, vT, *scratch), scale, (early, late))
         place(c, out_send.at[o_slot], lambda h: [
@@ -528,6 +524,7 @@
 
             @pl.when(fin & (n_fin >= LAG))
             def _():
+                fetch_sums(n_fin - LAG)
                 merge(n_fin - LAG)
         return 0
 

time: 431 us -> 432 us (level); the launches traced: 425 us -> 431 us
  Pallas kernels: 425 us -> 431 us
    pallas_call x1, Pallas kernels: 408 us -> 414 us  [local_attn(): pl.pallas_call(kernel, out_shape=(q_shape, q_shape, k_shape, k_shape, joi...]
where the time goes in v8:
time: 432 us; the launch traced here: 431 us
  Pallas kernels  431 us (100%)
    pallas_call x1, Pallas kernels, local_attn(): pl.pallas_call(kernel, out_shape=(q_shape, q_shape, k_shape, k_shape, joi...  414 us
    pallas_call x1, Pallas kernels, local_attn(): pl.pallas_call(finish_kernel, out_shape=(q_shape, q_shape, joined, joined...  16.5 us

profile of v8, /device:TPU:5, one launch (start us, length us, event | category | flops | bytes accessed | tf_op | source)
XLA Modules:
  0.0 431.4 jit_solution(16992109245160513673)
XLA Ops:
  0.6 414.2 %pair_attention.1 = (bf16[16,6,384,128]{3,2,1,0:T(8,128)(2,1)}, bf16[16,6,384,128]{3,2,1,0:T(8,128)(2,1)}, bf16[16,2,384,128]{3,2,1,0:T(8,128)(2,1)}, bf16[16,2,...) custom-call(bf16[16,6,384,128]{3,2,1,0:T(8,128)(2,1)} %bitcast.8, ...), custom_call_target="tpu_custom_call" | custom-call | tf_op jit(solution)/shard_map/pair_attention/pallas_call | solution.py:654
  414.8 16.5 %finish.1 = (bf16[16,6,384,128]{3,2,1,0:T(8,128)(2,1)}, bf16[16,6,384,128]{3,2,1,0:T(8,128)(2,1)}, bf16[16,768,128]{2,1,0:T(8,128)(2,1)}, bf16[16,768,128]{2,1,0:T(8,128)(2,1)}) custom-call(bf16[16,6,384,128]{3,2,1,0:T(8,128)(2,1)} %get-tuple-element.12.o, bf16[16,6,384,128]{3,2,1,0:T(8,128)(2,1)} %get-tuple-element.13.dq, ...), custom_call_target="tpu_custom_call" | custom-call | tf_op jit(solution)/shard_map/finish/pallas_call | solution.py:678
